TPU v7x, 32 devices: a whole 2x2x4 slice. The times are simulated.
32 devices in a mesh: lat: 16 (over z, y, x), lev: 2 (over core).
Axes of the slice: x: 2, y: 2, z: 4, core: 2. Of those that a mesh axis runs over, the one named last changes fastest.
Arguments:
- fields: float32 [160, 3, 16, 2560], P('lat', None, 'lev'), may hold values from 0.1 to 5
- lat_fraction: float32 [160], P('lat'), may hold values from 0 to 1
- lon_fraction: float32 [160], P('lat'), may hold values from 0 to 1
- lon_shift: int32 [160], P('lat'), may hold values from 0 to 2559
- departure_row: int32 [160], P('lat'), may hold values from 1 to 157, as said below
- extents: int32 [16, 2], P('lat'), may hold values from 1 to 4
Outputs:
- advected: float32 [160, 3, 16, 2560], P('lat', None, 'lev')
Inputs may be any that keep to these rules, and one draw needn't show every extreme that they name: departure_row[r] lies within 39 rows of r.
All inputs are finite; a program needn't handle non-finite values.
Results may differ from a plain program's by a relative error of at most 0.0003.
Values sent between devices are 32-bit elements; how exact they have to be, the bound alone decides.
No kernel may reach another device: no remote copies, remote signals or barrier semaphores. Data moves between devices by JAX's collectives and lax.ppermute only.
A program may use at most 128 MiB of HBM per device.

v0:
```python
import math

import jax
import jax.numpy as jnp
from jax import lax
from jax.sharding import PartitionSpec as P

REACH = 4


def from_behind(block, axis, distance):
    devices = range(lax.axis_size(axis))
    route = [(i - distance, i) for i in devices if i - distance in devices]
    return lax.ppermute(block, axis, route)


def cubic_weights(fraction):
    return jnp.stack(
        [
            -fraction * (fraction - 1.0) * (fraction - 2.0) / 6.0,
            (fraction + 1.0) * (fraction - 1.0) * (fraction - 2.0) / 2.0,
            -(fraction + 1.0) * fraction * (fraction - 2.0) / 2.0,
            (fraction + 1.0) * fraction * (fraction - 1.0) / 6.0,
        ]
    )


def along_lon(column, lon_w, shift_value):
    lon_count = column.shape[-1]
    doubled = jnp.concatenate([column, column], axis=-1)
    result = jnp.zeros_like(column)
    for offset in range(4):
        first = (shift_value + offset - 1) % lon_count
        result = result + lon_w[offset] * lax.dynamic_slice_in_dim(doubled, first, lon_count, 2)
    return result


def per_device(fields, lat_fraction, lon_fraction, lon_shift, departure_row, extents):
    row_count = fields.shape[0]
    band_index = lax.axis_index("lat")
    total_rows = lax.axis_size("lat") * row_count
    first_row = band_index * row_count
    north_bands = []
    south_bands = []
    for distance in range(1, REACH + 1):
        north_bands.insert(0, from_behind(fields, "lat", distance))
        south_bands.append(from_behind(fields, "lat", -distance))
    padded = jnp.concatenate(north_bands + [fields] + south_bands, axis=0)
    low_bound = first_row - extents[0, 0] * row_count + 1
    high_bound = first_row + row_count - 3 + extents[0, 1] * row_count
    departure = jnp.clip(jnp.clip(departure_row, low_bound, high_bound), 1, total_rows - 3)
    local_start = departure - 1 - (first_row - REACH * row_count)

    def one_row(inputs):
        start_value, lat_t, lon_t, shift_value = inputs
        row_block = lax.dynamic_slice_in_dim(padded, start_value, 4, 0)
        lat_w = cubic_weights(lat_t)
        column = (
            lat_w[0] * row_block[0]
            + lat_w[1] * row_block[1]
            + lat_w[2] * row_block[2]
            + lat_w[3] * row_block[3]
        )
        return along_lon(column, cubic_weights(lon_t), shift_value)

    moved = lax.map(one_row, (local_start, lat_fraction, lon_fraction, lon_shift))
    row_ids = first_row + jnp.arange(row_count, dtype=jnp.int32)
    area = jnp.cos(math.pi * (row_ids.astype(jnp.float32) + 0.5) / total_rows - math.pi / 2.0)
    local_before = jnp.sum(area[:, None, None, None] * fields, axis=(0, 2, 3))
    local_after = jnp.sum(area[:, None, None, None] * moved, axis=(0, 2, 3))
    mass_before, mass_after = lax.psum((local_before, local_after), ("lat", "lev"))
    return moved * (mass_before / mass_after)[None, :, None, None]


def solution(mesh):
    return jax.shard_map(
        per_device,
        mesh=mesh,
        in_specs=(
            P("lat", None, "lev", None),
            P("lat"),
            P("lat"),
            P("lat"),
            P("lat"),
            P("lat", None),
        ),
        out_specs=P("lat", None, "lev", None),
        check_vma=False,
    )
```

profile of v0, /device:TPU:0, one launch (start us, length us, event | category | flops | bytes accessed | tf_op | source)
XLA Modules:
  0.0 528.6 jit_solution(7406664660782324728)
XLA Ops:
  0.0 6.4 %collective-permute-start = (f32[10,3,8,2560]{3,2,1,0:T(8,128)}, f32[10,3,8,2560]{3,2,1,0:T(8,128)}, u32[]{:S(2)}, u32[]{:S(2)}) collective-permute-start(f32[10,3,8,2560]{3,2,1,0:T(8,128)} %param.8), channel_id=1, source_target_pairs={{0,8},{2,10},{4,12},{6,14},{8,16},{10,18},{12,20},{14,22},{16,24},... | collective-permute-start | bytes 7372808 | tf_op jit(solution)/shard_map/ppermute | solution.py:14
  6.4 5.8 %collective-permute-start.1 = (f32[10,3,8,2560]{3,2,1,0:T(8,128)}, f32[10,3,8,2560]{3,2,1,0:T(8,128)}, u32[]{:S(2)}, u32[]{:S(2)}) collective-permute-start(f32[10,3,8,2560]{3,2,1,0:T(8,128)} %param.8), channel_id=1, source_target_pairs={{0,6},{2,8},{4,10},{6,12},{8,14},{10,16},{12,18},{14,20},{16,22},{... | collective-permute-start | bytes 7372808 | tf_op jit(solution)/shard_map/ppermute | solution.py:14
  12.2 3.4 collective-permute-start.2
  15.6 2.8 collective-permute-start.3
  18.4 1.3 collective-permute-start.4
  19.7 1.3 fusion.17
  22.3 0.7 add_subtract_fusion
  23.0 34.9 %collective-permute-done = f32[10,3,8,2560]{3,2,1,0:T(8,128)} collective-permute-done((f32[10,3,8,2560]{3,2,1,0:T(8,128)}, f32[10,3,8,2560]{3,2,1,0:T(8,128)}, u32[]{:S(2)}, u32[]{:S(2)}) %collective-permute-start) | collective-permute-done | bytes 2457632 | tf_op jit(solution)/shard_map/ppermute | solution.py:14
  57.9 1.3 collective-permute-start.5
  59.2 1.9 constant_dynamic-update-slice_fusion.8
  61.0 159.4 %collective-permute-done.1 = f32[10,3,8,2560]{3,2,1,0:T(8,128)} collective-permute-done((f32[10,3,8,2560]{3,2,1,0:T(8,128)}, f32[10,3,8,2560]{3,2,1,0:T(8,128)}, u32[]{:S(2)}, u32[]{:S(2)}) %collective-permute-start.1) | collective-permute-done | bytes 2457632 | tf_op jit(solution)/shard_map/ppermute | solution.py:14
  220.4 1.3 collective-permute-start.6
  221.7 1.9 constant_dynamic-update-slice_fusion.7
  223.5 1.0 collective-permute-done.2
  224.5 1.3 collective-permute-start.7
  225.8 1.9 constant_dynamic-update-slice_fusion.6
  227.7 43.9 %collective-permute-done.3 = f32[10,3,8,2560]{3,2,1,0:T(8,128)} collective-permute-done((f32[10,3,8,2560]{3,2,1,0:T(8,128)}, f32[10,3,8,2560]{3,2,1,0:T(8,128)}, u32[]{:S(2)}, u32[]{:S(2)}) %collective-permute-start.3) | collective-permute-done | bytes 2457632 | tf_op jit(solution)/shard_map/ppermute | solution.py:14
  271.6 1.9 constant_dynamic-update-slice_fusion.5
  273.7 1.9 constant_dynamic-update-slice_fusion.3
  276.0 4.1 collective-permute-done.7
  280.3 7.3 %copy-done.1 = f32[90,3,8,2560]{3,2,1,0:T(8,128)} copy-done((f32[90,3,8,2560]{3,2,1,0:T(8,128)}, f32[90,3,8,2560]{3,2,1,0:T(8,128)S(1)}, u32[]{:S(2)}) %copy-start.1) | copy-done | bytes 22118424
  287.6 165.5 %while.15 = (s32[]{:T(128)}, f32[10,3,8,2560]{3,2,1,0:T(8,128)S(1)}, f32[10]{0:T(128)S(1)}, f32[10]{0:T(128)S(1)}, s32[10]{0:T(128)S(1)}, /*index=5*/f32[90,3,8,...) while((s32[]{:T(128)}, ...), condition=%wide.region_1.2_spmd, body=%wide.region_0.1_spmd.sunk | while | flops 1106001 | bytes 1721515 | solution.py:66
  292.0 0.7 dynamic_slice.169
  294.6 1.4 fusion.20
  296.0 0.7 dynamic_slice.168
  299.2 0.7 dynamic_slice.171
  308.6 0.7 dynamic_slice.169
  311.1 1.4 fusion.20
  312.5 0.7 dynamic_slice.168
  315.7 0.7 dynamic_slice.171
  325.1 0.7 dynamic_slice.169
  327.7 1.4 fusion.20
  329.0 0.7 dynamic_slice.168
  332.3 0.7 dynamic_slice.171
  341.7 0.7 dynamic_slice.169
  344.2 1.4 fusion.20
  345.6 0.7 dynamic_slice.168
  348.8 0.7 dynamic_slice.171
  358.2 0.7 dynamic_slice.169
  360.8 1.4 fusion.20
  362.1 0.7 dynamic_slice.168
  365.4 0.7 dynamic_slice.171
  374.8 0.7 dynamic_slice.169
  377.3 1.4 fusion.20
  378.7 0.7 dynamic_slice.168
  381.9 0.7 dynamic_slice.171
  391.3 0.7 dynamic_slice.169
  393.9 1.4 fusion.20
  395.2 0.7 dynamic_slice.168
  398.5 0.7 dynamic_slice.171
  407.9 0.7 dynamic_slice.169
  410.4 1.4 fusion.20
  411.8 0.7 dynamic_slice.168
  415.0 0.7 dynamic_slice.171
  424.4 0.7 dynamic_slice.169
  426.9 1.4 fusion.20
  428.3 0.7 dynamic_slice.168
  431.6 0.7 dynamic_slice.171
  441.0 0.7 dynamic_slice.169
  443.5 1.4 fusion.20
  444.9 0.7 dynamic_slice.168
  453.1 2.3 multiply_reduce_fusion
  455.4 71.3 %all-reduce = (f32[3]{0:T(128)S(1)}, f32[3]{0:T(128)S(1)}) all-reduce(f32[3]{0:T(128)S(1)} %get-tuple-element.190, f32[3]{0:T(128)S(1)} %get-tuple-element.189), channel_id=1, replica_groups=mesh['lat'=16,'lev'=2] {'lat','lev'}, use_global_device_ids=true, to_apply=%region_3.4 | all-reduce | flops 6 | bytes 48 | tf_op jit(solution)/shard_map/psum | solution.py:71
  526.8 1.8 broadcast_multiply_fusion
  (40 shorter events, 14.1 us)
Async XLA Ops:
  0.0 57.9 %collective-permute-start = (f32[10,3,8,2560]{3,2,1,0:T(8,128)}, f32[10,3,8,2560]{3,2,1,0:T(8,128)}, u32[]{:S(2)}, u32[]{:S(2)}) collective-permute-start(f32[10,3,8,2560]{3,2,1,0:T(8,128)} %param.8), channel_id=1, source_target_pairs={{0,8},{2,10},{4,12},{6,14},{8,16},{10,18},{12,20},{14,22},{16,24},... | collective-permute-start | bytes 7372808 | tf_op jit(solution)/shard_map/ppermute | solution.py:14
  6.4 214.0 %collective-permute-start.1 = (f32[10,3,8,2560]{3,2,1,0:T(8,128)}, f32[10,3,8,2560]{3,2,1,0:T(8,128)}, u32[]{:S(2)}, u32[]{:S(2)}) collective-permute-start(f32[10,3,8,2560]{3,2,1,0:T(8,128)} %param.8), channel_id=1, source_target_pairs={{0,6},{2,8},{4,10},{6,12},{8,14},{10,16},{12,18},{14,20},{16,22},{... | collective-permute-start | bytes 7372808 | tf_op jit(solution)/shard_map/ppermute | solution.py:14
  12.2 212.3 %collective-permute-start.2 = (f32[10,3,8,2560]{3,2,1,0:T(8,128)}, f32[10,3,8,2560]{3,2,1,0:T(8,128)}, u32[]{:S(2)}, u32[]{:S(2)}) collective-permute-start(f32[10,3,8,2560]{3,2,1,0:T(8,128)} %param.8), channel_id=1, source_target_pairs={{0,4},{2,6},{4,8},{6,10},{8,12},{10,14},{12,16},{14,18},{16,20},{1... | collective-permute-start | bytes 7372808 | tf_op jit(solution)/shard_map/ppermute | solution.py:14
  15.6 256.0 %collective-permute-start.3 = (f32[10,3,8,2560]{3,2,1,0:T(8,128)}, f32[10,3,8,2560]{3,2,1,0:T(8,128)}, u32[]{:S(2)}, u32[]{:S(2)}) collective-permute-start(f32[10,3,8,2560]{3,2,1,0:T(8,128)} %param.8), channel_id=1, source_target_pairs={{0,2},{2,4},{4,6},{6,8},{8,10},{10,12},{12,14},{14,16},{16,18},{18... | collective-permute-start | bytes 7372808 | tf_op jit(solution)/shard_map/ppermute | solution.py:14
  18.4 255.3 %collective-permute-start.4 = (f32[10,3,8,2560]{3,2,1,0:T(8,128)}, f32[10,3,8,2560]{3,2,1,0:T(8,128)}, u32[]{:S(2)}, u32[]{:S(2)}) collective-permute-start(f32[10,3,8,2560]{3,2,1,0:T(8,128)} %param.8), channel_id=1, source_target_pairs={{2,0},{4,2},{6,4},{8,6},{10,8},{12,10},{14,12},{16,14},{18,16},{20... | collective-permute-start | bytes 7372808 | tf_op jit(solution)/shard_map/ppermute | solution.py:14
  23.0 197.4 %copy-start = (f32[10,3,8,2560]{3,2,1,0:T(8,128)S(1)}, f32[10,3,8,2560]{3,2,1,0:T(8,128)}, u32[]{:S(2)}) copy-start(f32[10,3,8,2560]{3,2,1,0:T(8,128)} %param.8) | copy-start | bytes 7372804
  57.9 217.7 %collective-permute-start.5 = (f32[10,3,8,2560]{3,2,1,0:T(8,128)}, f32[10,3,8,2560]{3,2,1,0:T(8,128)S(1)}, u32[]{:S(2)}, u32[]{:S(2)}) collective-permute-start(f32[10,3,8,2560]{3,2,1,0:T(8,128)} %param.8), channel_id=1, source_target_pairs={{4,0},{6,2},{8,4},{10,6},{12,8},{14,10},{16,12},{18,14},{20,16},{2... | collective-permute-start | bytes 7372808 | tf_op jit(solution)/shard_map/ppermute | solution.py:14
  220.4 55.4 %collective-permute-start.6 = (f32[10,3,8,2560]{3,2,1,0:T(8,128)S(1)}, f32[10,3,8,2560]{3,2,1,0:T(8,128)S(1)}, u32[]{:S(2)}, u32[]{:S(2)}) collective-permute-start(f32[10,3,8,2560]{3,2,1,0:T(8,128)S(1)} %copy-done), channel_id=1, source_target_pairs={{6,0},{8,2},{10,4},{12,6},{14,8},{16,10},{18,12},{20,14},{22,16},{... | collective-permute-start | bytes 7372808 | tf_op jit(solution)/shard_map/ppermute | solution.py:14
  224.5 55.6 %collective-permute-start.7 = (f32[10,3,8,2560]{3,2,1,0:T(8,128)S(1)}, f32[10,3,8,2560]{3,2,1,0:T(8,128)S(1)}, u32[]{:S(2)}, u32[]{:S(2)}) collective-permute-start(f32[10,3,8,2560]{3,2,1,0:T(8,128)S(1)} %copy-done), channel_id=1, source_target_pairs={{8,0},{10,2},{12,4},{14,6},{16,8},{18,10},{20,12},{22,14},{24,16},... | collective-permute-start | bytes 7372808 | tf_op jit(solution)/shard_map/ppermute | solution.py:14
  276.0 11.7 %copy-start.2 = (f32[10]{0:T(128)S(1)}, f32[10]{0:T(128)}, u32[]{:S(2)}) copy-start(f32[10]{0:T(128)} %param.10) | copy-start | bytes 124
  276.0 11.7 %copy-start.3 = (f32[10]{0:T(128)S(1)}, f32[10]{0:T(128)}, u32[]{:S(2)}) copy-start(f32[10]{0:T(128)} %param.9) | copy-start | bytes 124
  276.0 11.6 %copy-start.4 = (s32[10]{0:T(128)S(1)}, s32[10]{0:T(128)}, u32[]{:S(2)}) copy-start(s32[10]{0:T(128)} %param.11) | copy-start | bytes 124
  280.3 7.3 %copy-start.1 = (f32[90,3,8,2560]{3,2,1,0:T(8,128)}, f32[90,3,8,2560]{3,2,1,0:T(8,128)S(1)}, u32[]{:S(2)}) copy-start(f32[90,3,8,2560]{3,2,1,0:T(8,128)S(1)} %constant_dynamic-update-slice_fusion) | copy-start | bytes 66355204
where the time goes:
time: 531 us; the launch traced here: 529 us
  waiting for transfers between devices  243 us (46%)
  loops' own time  119 us (22%)
  blocking collectives  71.3 us (13%)
  local copies, waits for them, and re-layouts  44.8 us (8%)
  other arithmetic  24.8 us (5%)
  starting transfers between devices  23.5 us (4%)
    ppermute x8, waiting for transfers between devices, from_behind(): return lax.ppermute(block, axis, route)  243 us
    another operation x1, loops' own time, per_device(): lax.map(one_row, (local_start, lat_fraction, lon_fraction, lon_shift))  119 us
    psum x1, blocking collectives, per_device(): lax.psum((local_before, local_after), ('lat', 'lev'))  71.3 us
    dynamic_slice x40, local copies, waits for them, and re-layouts, per_device(): lax.map(one_row, (local_start, lat_fraction, lon_fraction, lon_shift))  26.1 us
    ppermute x8, starting transfers between devices, from_behind(): return lax.ppermute(block, axis, route)  23.5 us
    unnamed x18, local copies, waits for them, and re-layouts  17.2 us
    add x10, other arithmetic, one_row(): lat_w[0] * row_block[0] + lat_w[1] * row_block[1] + lat_w[2] * row_block[2]  13.8 us
  transfers between devices with their start and end apart: 8, of which 5 were waited for; matrix products, arithmetic and copies ran while one was open for 2% of the time, Pallas kernels for 0%

commit v1 on v0

v1 whole, which is shorter than its diff:
```python
import functools
import math

import jax
import jax.numpy as jnp
from jax import lax
from jax.experimental import pallas as pl
from jax.experimental.pallas import tpu as pltpu
from jax.sharding import PartitionSpec as P


REACH = 4
LANES = 128
VMEM_LIMIT = 12 * 1024 * 1024
START_LIMIT = 60 * 1024 * 1024


def flip(mask):
    return lambda me: me ^ mask


def stay(me):
    return me


def across(me):
    return ((me + REACH) ^ REACH) - REACH


def onward(me):
    return me + REACH * (1 - (me & 2))


def back(me):
    return me - REACH * (1 - (me & 2))


def side(me):
    return back(me) ^ 2


def send(block, place):
    devices = range(lax.axis_size("lat"))
    route = [(i, place(i)) for i in devices if place(i) in devices]
    return lax.ppermute(block, "lat", route)


def cubic_weights(t):
    return (
        t * (t - 1.0) * (t - 2.0) * (-1.0 / 6.0),
        (t + 1.0) * (t - 1.0) * (t - 2.0) * 0.5,
        (t + 1.0) * t * (t - 2.0) * -0.5,
        (t + 1.0) * t * (t - 1.0) * (1.0 / 6.0),
    )


def vmem():
    return pl.BlockSpec(memory_space=pltpu.VMEM)


def smem():
    return pl.BlockSpec(memory_space=pltpu.SMEM)


def hbm():
    return pl.BlockSpec(memory_space=pltpu.HBM)


def from_hbm(array):
    return pltpu.with_memory_space_constraint(array, pltpu.HBM)


def cost(operands, results, flops):
    size = math.prod(results[0].shape)
    count = len(operands) + len(results)
    return pl.CostEstimate(flops=flops * size, bytes_accessed=4 * size * count, transcendentals=0)


def start_kernel(departure_row, lat_fraction, lon_fraction, extents, fields, *refs):
    parts, plan = refs[:-11], refs[-11]
    departure_s, lat_s, lon_s, extents_s, held, ready, tile_s = refs[-10:-3]
    sems, in_sems, out_sems = refs[-3:]
    row_count, field_count, lev_count, lon_count = fields.shape
    tile_count = lon_count // LANES
    scalars = (departure_row, lat_fraction, lon_fraction, extents)
    copies = [
        pltpu.make_async_copy(source, target, sems.at[k])
        for k, (source, target) in enumerate(zip(scalars, (departure_s, lat_s, lon_s, extents_s)))
    ]
    rows = [pltpu.make_async_copy(fields.at[r], held.at[r], in_sems.at[r]) for r in range(row_count)]
    for copy in copies + rows:
        copy.start()
    for copy in copies:
        copy.wait()
    first_row = lax.axis_index("lat") * row_count
    low_bound = first_row - extents_s[0, 0] * row_count + 1
    high_bound = first_row + row_count - 3 + extents_s[0, 1] * row_count
    last = lax.axis_size("lat") * row_count - 3
    at = lax.broadcasted_iota(jnp.int32, (lev_count, LANES), 1)
    tile = jnp.zeros((lev_count, LANES), jnp.float32)
    for r in range(row_count):
        departure = jnp.clip(jnp.clip(departure_s[r], low_bound, high_bound), 1, last)
        tile = jnp.where(at == r, departure.astype(jnp.float32), tile)
        tile = jnp.where(at == row_count + r, lat_s[r], tile)
        tile = jnp.where(at == 2 * row_count + r, lon_s[r], tile)
    tile_s[...] = tile
    plan[0] = tile
    ships = []
    for f, part in enumerate(parts):
        ships.append(pltpu.make_async_copy(tile_s, part.at[row_count * tile_count], out_sems.at[f, row_count]))
    for r in range(row_count):
        rows[r].wait()
        for ship in ships[-field_count:]:
            ship.start()
        for f, part in enumerate(parts):
            for n in range(tile_count):
                ready[f, r * tile_count + n] = held[r, f, :, n * LANES : (n + 1) * LANES]
            span = pl.ds(r * tile_count, tile_count)
            ships.append(pltpu.make_async_copy(ready.at[f, span], part.at[span], out_sems.at[f, r]))
    for ship in ships[-field_count:]:
        ship.start()
    for ship in ships:
        ship.wait()


def start(departure_row, lat_fraction, lon_fraction, extents, fields):
    row_count, field_count, lev_count, lon_count = fields.shape
    tiles = row_count * lon_count // LANES
    part = jax.ShapeDtypeStruct((tiles + 1, lev_count, LANES), jnp.float32)
    plan = jax.ShapeDtypeStruct((1, lev_count, LANES), jnp.float32)
    return pl.pallas_call(
        start_kernel,
        out_shape=[part] * field_count + [plan],
        in_specs=[hbm()] * 5,
        out_specs=[hbm()] * field_count + [vmem()],
        scratch_shapes=[
            pltpu.SMEM(departure_row.shape, jnp.int32),
            pltpu.SMEM(lat_fraction.shape, jnp.float32),
            pltpu.SMEM(lon_fraction.shape, jnp.float32),
            pltpu.SMEM(extents.shape, jnp.int32),
            pltpu.VMEM(fields.shape, jnp.float32),
            pltpu.VMEM((field_count, tiles, lev_count, LANES), jnp.float32),
            pltpu.VMEM((lev_count, LANES), jnp.float32),
            pltpu.SemaphoreType.DMA((4,)),
            pltpu.SemaphoreType.DMA((row_count,)),
            pltpu.SemaphoreType.DMA((field_count, row_count + 1)),
        ],
        compiler_params=pltpu.CompilerParams(vmem_limit_bytes=START_LIMIT),
        cost_estimate=cost([part] * field_count, [part] * field_count, 3),
    )(departure_row, lat_fraction, lon_fraction, extents, fields)


def sums_kernel(row_count, *refs):
    parts, mine = refs[:-1], refs[-1]
    tile_count = parts[0].shape[0] // row_count
    at = lax.broadcasted_iota(jnp.int32, (1, LANES), 1)
    line = parts[0][row_count * tile_count][:1]
    for r in range(row_count):
        for f, part in enumerate(parts):
            tiles = [part[r * tile_count + n] for n in range(tile_count)]
            while len(tiles) > 1:
                tiles = [sum(tiles[k : k + 2]) for k in range(0, len(tiles), 2)]
            line = jnp.where(at == 3 * row_count + r * len(parts) + f, jnp.sum(tiles[0]), line)
    mine[...] = jnp.broadcast_to(line[None], mine.shape)


def exchange(parts, row_count):
    copies = lax.axis_size("lat") * lax.axis_size("lev")
    mine = pl.pallas_call(
        functools.partial(sums_kernel, row_count),
        out_shape=jax.ShapeDtypeStruct((copies, 1, LANES), jnp.float32),
        in_specs=[vmem()] * len(parts),
        out_specs=vmem(),
        compiler_params=pltpu.CompilerParams(vmem_limit_bytes=VMEM_LIMIT),
        cost_estimate=cost(parts, parts[:1], 3),
    )(*parts)
    return lax.all_to_all(mine, ("lat", "lev"), 0, 0, tiled=True)


def collect_kernel(*refs):
    parts, tiles, sems = refs[:-2], refs[-2], refs[-1]
    copies = [
        pltpu.make_async_copy(part.at[part.shape[0] - 1], tiles.at[k], sems.at[k])
        for k, part in enumerate(parts)
    ]
    for copy in copies:
        copy.start()
    for copy in copies:
        copy.wait()


def collect(parts):
    return pl.pallas_call(
        collect_kernel,
        out_shape=jax.ShapeDtypeStruct((len(parts),) + parts[0].shape[1:], jnp.float32),
        in_specs=[hbm()] * len(parts),
        out_specs=vmem(),
        scratch_shapes=[pltpu.SemaphoreType.DMA((len(parts),))],
        compiler_params=pltpu.CompilerParams(vmem_limit_bytes=VMEM_LIMIT),
        cost_estimate=pl.CostEstimate(flops=1000, bytes_accessed=8000, transcendentals=0),
    )(*parts)


def add_bands(plan, band_refs, band_ids, row_count, out_ref):
    tile_count = out_ref.shape[0] // row_count

    def row(r, carry):
        first = plan[0, r].astype(jnp.int32) - 1
        weights = cubic_weights(plan[0, row_count + r])
        for ref, band in zip(band_refs, band_ids):
            local = first - band * row_count

            @pl.when((local > -4) & (local < row_count))
            def _():
                total = out_ref[pl.ds(r * tile_count, tile_count)]
                for a in range(4):
                    index = local + a
                    inside = (index >= 0) & (index < row_count)
                    weight = jnp.where(inside, weights[a], 0.0)
                    index = jnp.clip(index, 0, row_count - 1)
                    total = total + weight * ref[pl.ds(index * tile_count, tile_count)]
                out_ref[pl.ds(r * tile_count, tile_count)] = total

        return carry

    lax.fori_loop(0, row_count, row, 0)


def combine_kernel(row_count, jobs, *refs):
    me = lax.axis_index("lat")
    outs = refs[len(refs) - len(jobs) :]
    for (bands, places, plan, line, seed), out in zip(jobs, outs):
        out[...] = jnp.zeros_like(out) if seed is None else refs[seed][pl.ds(0, out.shape[0])]
        band_ids = [place(me) for place in places]
        add_bands(refs[plan].at[line(me)], [refs[b] for b in bands], band_ids, row_count, out)


def combine(row_count, *jobs):
    scalars, arrays = [], []

    def index(array, known):
        for k, other in enumerate(known):
            if other is array:
                return k
        known.append(array)
        return len(known) - 1

    kept = []
    for bands, places, (plan, line), *seed in jobs:
        held = [index(b, arrays) for b in bands]
        kept.append((held, places, index(plan, scalars), line, index(seed[0], arrays) if seed else None))
    shift = len(scalars)
    kept = [
        ([b + shift for b in held], places, plan, line, None if seed is None else seed + shift)
        for held, places, plan, line, seed in kept
    ]
    tiles, lev_count, _ = jobs[0][0][0].shape
    outs = [jax.ShapeDtypeStruct((tiles - 1, lev_count, LANES), jnp.float32)] * len(jobs)
    return pl.pallas_call(
        functools.partial(combine_kernel, row_count, kept),
        out_shape=outs,
        in_specs=[smem()] * len(scalars) + [vmem()] * len(arrays),
        out_specs=[vmem()] * len(outs),
        compiler_params=pltpu.CompilerParams(vmem_limit_bytes=VMEM_LIMIT),
        cost_estimate=cost(arrays, outs, 8 * len(outs)),
    )(*scalars, *arrays)


def finish_kernel(split, plan, shifts, ratio, *refs):
    pieces = refs[: sum(len(held) for _, held in split)]
    out, kept, twice, ready, plan_s, shifts_s, ratio_s, scalar_sems, in_sems, sems = refs[-10:]
    row_count, lev_count, lon_count = ready.shape[1:]
    tile_count = lon_count // LANES
    group = twice.shape[0]
    lane = lax.broadcasted_iota(jnp.int32, (lev_count, LANES), 1)
    scalars = [
        pltpu.make_async_copy(source, target, scalar_sems.at[k])
        for k, (source, target) in enumerate(zip((plan, shifts, ratio), (plan_s, shifts_s, ratio_s)))
    ]

    def fetch(p, step):
        span = pl.ds(step * group * tile_count, group * tile_count)
        return pltpu.make_async_copy(pieces[p].at[span], kept.at[p, span], in_sems.at[p, step])

    for copy in scalars:
        copy.start()
    for _, held in split:
        for step in range(row_count // group):
            for p in held:
                fetch(p, step).start()
    for copy in scalars:
        copy.wait()

    for k, (field, held) in enumerate(split):

        def ship(r):
            return pltpu.make_async_copy(ready.at[k, r], out.at[r, field], sems.at[k, r])

        def rows(step, carry):
            for p in held:
                fetch(p, step).wait()
            for u in range(group):
                span = pl.ds((step * group + u) * tile_count, tile_count)
                column = kept[held[0], span]
                for p in held[1:]:
                    column = column + kept[p, span]
                twice[u, :tile_count] = column
                twice[u, tile_count : 2 * tile_count] = column
                twice[u, 2 * tile_count] = column[0]
            for u in range(group):
                r = step * group + u
                weights = cubic_weights(plan_s[0, 0, 2 * row_count + r])
                base = shifts_s[r] - 1
                base = jnp.where(base < 0, base + lon_count, base)
                moved = [None] * tile_count
                for tap in range(4):
                    first = (base + tap) // LANES
                    turn = (base + tap) % LANES
                    weight = weights[tap] * ratio_s[field]
                    keep = lane < LANES - turn
                    shift = jnp.where(turn == 0, 0, LANES - turn)
                    tiles = [pltpu.roll(twice[u, first + n], shift, axis=1) for n in range(tile_count + 1)]
                    for n in range(tile_count):
                        term = weight * jnp.where(keep, tiles[n], tiles[n + 1])
                        moved[n] = term if tap == 0 else moved[n] + term
                for n in range(tile_count):
                    ready[k, r, :, n * LANES : (n + 1) * LANES] = moved[n]

            @pl.when(step > 0)
            def _():
                for u in range(group):
                    ship((step - 1) * group + u).start()

            return carry

        lax.fori_loop(0, row_count // group, rows, 0)
        for u in range(group):
            ship(row_count - group + u).start()
    for k, (field, _) in enumerate(split):
        for r in range(row_count):
            pltpu.make_async_copy(ready.at[k, r], out.at[r, field], sems.at[k, r]).wait()


def finish(plan, shifts, ratio, pieces, out_shape, out=None):
    row_count, _, lev_count, lon_count = out_shape
    given = [] if out is None else [out]
    group = next(g for g in (5, 4, 3, 2, 1) if row_count % g == 0)
    flat, split = [], []
    for field, parts in pieces.items():
        split.append((field, tuple(range(len(flat), len(flat) + len(parts)))))
        flat += parts
    return pl.pallas_call(
        functools.partial(finish_kernel, split),
        out_shape=jax.ShapeDtypeStruct(out_shape, jnp.float32),
        in_specs=[hbm()] * (3 + len(flat) + len(given)),
        out_specs=hbm(),
        input_output_aliases={3 + len(flat): 0} if given else {},
        scratch_shapes=[
            pltpu.VMEM((len(flat),) + flat[0].shape, jnp.float32),
            pltpu.VMEM((group, 2 * lon_count // LANES + 1, lev_count, LANES), jnp.float32),
            pltpu.VMEM((len(split), row_count, lev_count, lon_count), jnp.float32),
            pltpu.SMEM(plan.shape, plan.dtype),
            pltpu.SMEM(shifts.shape, shifts.dtype),
            pltpu.SMEM(ratio.shape, ratio.dtype),
            pltpu.SemaphoreType.DMA((3,)),
            pltpu.SemaphoreType.DMA((len(flat), row_count // group)),
            pltpu.SemaphoreType.DMA((len(split), row_count)),
        ],
        compiler_params=pltpu.CompilerParams(vmem_limit_bytes=VMEM_LIMIT),
        cost_estimate=cost(flat, flat[:1], 60 * len(split)),
    )(plan, shifts, ratio, *flat, *given)


def mass_ratio(table, row_count, field_count):
    band_count, lev_size = lax.axis_size("lat"), lax.axis_size("lev")
    total_rows = band_count * row_count
    parts = table.reshape(band_count, lev_size, -1)
    columns = [parts[:, 0, k * row_count : (k + 1) * row_count].reshape(total_rows) for k in range(3)]
    first = columns[0].astype(jnp.int32) - 1
    lat_w = cubic_weights(columns[1])
    lon_w = cubic_weights(columns[2])
    sums = parts[:, :, 3 * row_count : (3 + field_count) * row_count].sum(1).reshape(total_rows, field_count)
    row_ids = jnp.arange(total_rows, dtype=jnp.int32)
    area = jnp.cos(math.pi * (row_ids.astype(jnp.float32) + 0.5) / total_rows - math.pi / 2.0)
    gain = area * (lon_w[0] + lon_w[1] + lon_w[2] + lon_w[3])
    hit = jnp.zeros((total_rows, total_rows), jnp.float32)
    for a in range(4):
        hit = hit + jnp.where((first + a)[:, None] == row_ids[None, :], (gain * lat_w[a])[:, None], 0.0)
    after_w = hit.sum(0)
    before = (area[:, None] * sums).sum(0)
    after = (after_w[:, None] * sums).sum(0)
    return before / after


def one_step(fields, lat_fraction, lon_fraction, lon_shift, departure_row, extents):
    row_count, field_count = fields.shape[:2]
    near, middle, both = flip(1), flip(2), flip(3)
    even, odd = flip(REACH), across
    join = functools.partial(combine, row_count)
    f0, f1, f2, plan = start(departure_row, lat_fraction, lon_fraction, extents, fields)
    both_plan = send(plan, both)
    f2_middle = send(f2, middle)
    f0_even = send(f0, even)
    f0_odd = send(f0, odd)
    f1_near = send(f1, near)
    f1_middle = send(f1, middle)
    table = exchange([from_hbm(f) for f in (f0, f1, f2)], row_count)
    f2_even = send(f2, even)
    f2_odd = send(f2, odd)
    f1_both = send(f1_near, middle)
    f2_side = send(f2_middle, onward)

    f0, f1, f2 = (from_hbm(f) for f in (f0, f1, f2))
    plans = collect([f1_near, f2_middle, f0_even, f0_odd])
    near_plan, middle_plan = (plans, lambda me: 0), (plans, lambda me: 1)
    onward_plan = (plans, lambda me: jnp.where(onward(me) == even(me), 2, 3))
    back_plan = (plans, lambda me: jnp.where(back(me) == even(me), 2, 3))
    own_plan, far_plan = (plan, lambda me: 0), (both_plan, lambda me: 0)

    f0_all = [f0, f0_even, f0_odd], [stay, even, odd]
    (for_both,) = join((*f0_all, far_plan))
    f0_relay = send(for_both, near)
    (for_near,) = join((*f0_all, near_plan))
    f0_from_near = send(for_near, near)
    (for_middle,) = join((*f0_all, middle_plan, f0_relay))
    f0_from_middle = send(for_middle, middle)

    (for_back,) = join(([f1, f1_near], [stay, near], back_plan))
    f1_from_onward = send(for_back, back)
    f1_all = [f1, f1_near, f1_middle], [stay, near, middle]
    f1_early, f1_own = join((*f1_all, onward_plan), (*f1_all, own_plan))
    f2_all = [f2, f2_middle, f2_even, f2_odd], [stay, middle, even, odd]
    f2_early, f2_own = join((*f2_all, near_plan), (*f2_all, own_plan))
    (for_onward,) = join(([f1_both], [both], onward_plan, f1_early))
    f1_from_back = send(for_onward, onward)
    (f2_for_near,) = join(([f2_side], [side], near_plan, f2_early))
    f2_from_near = send(f2_for_near, near)
    (f0_own,) = join((*f0_all, own_plan, f0_from_near))
    (f1_own,) = join(([f1_both], [both], own_plan, f1_own))
    (f2_own,) = join(([f2_side], [side], own_plan, f2_own))

    ratio = mass_ratio(table, row_count, field_count)
    pieces = [f0_own, f0_from_middle], [f1_own, f1_from_onward, f1_from_back], [f2_own, f2_from_near]
    out = None
    for field, parts in enumerate(pieces):
        out = finish(plan, lon_shift, ratio, {field: parts}, fields.shape, out)
    return out


def solution(mesh):
    return jax.shard_map(
        one_step,
        mesh=mesh,
        in_specs=(
            P("lat", None, "lev", None),
            P("lat"),
            P("lat"),
            P("lat"),
            P("lat"),
            P("lat", None),
        ),
        out_specs=P("lat", None, "lev", None),
        check_vma=False,
    )
```

time: 531 us -> 119 us (0.22)
  waiting for transfers between devices: 243 us -> 46 us
  loops' own time: 119 us -> 0 us
  blocking collectives: 71.3 us -> 0 us
  local copies, waits for them, and re-layouts: 44.8 us -> 1.37 us
  Pallas kernels: 0 us -> 36.6 us
  other arithmetic: 24.8 us -> 0.59 us
  starting transfers between devices: 23.5 us -> 33.7 us
    ppermute x8 -> x16, waiting for transfers between devices: 243 us -> 34.5 us  [send(): return lax.ppermute(block, 'lat', route)]
    another operation x1 -> x0, loops' own time: 119 us -> none  [per_device(): lax.map(one_row, (local_start, lat_fraction, lon_fraction, lon_shift))]
    psum x1 -> x0, blocking collectives: 71.3 us -> none  [per_device(): lax.psum((local_before, local_after), ('lat', 'lev'))]
    pallas_call x0 -> x17, Pallas kernels: none -> 36.6 us  [the longest x11 20.2 us: combine(): pl.pallas_call(functools.partial(combine_kernel, row_count, kept), out_sh...]
    dynamic_slice x40 -> x0, local copies, waits for them, and re-layouts: 26.1 us -> none  [per_device(): lax.map(one_row, (local_start, lat_fraction, lon_fraction, lon_shift))]
    unnamed x18 -> x8, local copies, waits for them, and re-layouts: 17.2 us -> 0.94 us
    add x10 -> x0, other arithmetic: 13.8 us -> none  [one_row(): lat_w[0] * row_block[0] + lat_w[1] * row_block[1] + lat_w[2] * row_block[2]]
    all_to_all x0 -> x1, waiting for transfers between devices: none -> 11.5 us  [exchange(): return lax.all_to_all(mine, ('lat', 'lev'), 0, 0, tiled=True)]
  transfers between devices with their start and end apart: 8 -> 17, of which waited for: 5 -> 9; matrix products, arithmetic and copies ran while one was open for 2% -> 1% of each run, Pallas kernels for 0% -> 25%
where the time goes in v1:
time: 119 us
  waiting for transfers between devices  46 us (39%)
  Pallas kernels  36.6 us (31%)
  starting transfers between devices  33.7 us (28%)
  local copies, waits for them, and re-layouts  1.37 us (1%)
    ppermute x16, waiting for transfers between devices, send(): return lax.ppermute(block, 'lat', route)  34.5 us
    ppermute x16, starting transfers between devices, send(): return lax.ppermute(block, 'lat', route)  29 us
    pallas_call x11, Pallas kernels, combine(): pl.pallas_call(functools.partial(combine_kernel, row_count, kept), out_sh...  20.2 us
    all_to_all x1, waiting for transfers between devices, exchange(): return lax.all_to_all(mine, ('lat', 'lev'), 0, 0, tiled=True)  11.5 us
    pallas_call x3, Pallas kernels, finish(): pl.pallas_call(functools.partial(finish_kernel, split), out_shape=jax.Sha...  9.58 us
    all_to_all x1, starting transfers between devices, exchange(): return lax.all_to_all(mine, ('lat', 'lev'), 0, 0, tiled=True)  4.71 us
    pallas_call x1, Pallas kernels, start(): pl.pallas_call(start_kernel, out_shape=[part] * field_count + [plan], in_...  3.57 us
    pallas_call x1, Pallas kernels, exchange(): pl.pallas_call(functools.partial(sums_kernel, row_count), out_shape=jax.S...  2.5 us
  transfers between devices with their start and end apart: 17, of which 9 were waited for; matrix products, arithmetic and copies ran while one was open for 1% of the time, Pallas kernels for 25%

profile of v1, /device:TPU:0, one launch (start us, length us, event | category | flops | bytes accessed | tf_op | source)
XLA Modules:
  0.0 118.5 jit_solution(6755639499958642473)
XLA Ops:
  0.0 3.6 %shard_map.64 = (f32[201,8,128]{2,1,0:T(8,128)}, f32[201,8,128]{2,1,0:T(8,128)}, f32[201,8,128]{2,1,0:T(8,128)}, f32[1,8,128]{2,1,0:T(8,128)}) custom-call(s32[10]{0:T(128)} %departure_row.1, f32[10]{0:T(128)} %lat_fraction.1, f32[10]{0:T(128)} %lon_fraction.1, s32[1,2]{1,0:T(1,128)} %extents.1, f32[10,3,8,2560]{3,2,1,0:T(8,128)} %fields.1), custom_call_target="tpu_custom_call" | custom-call | flops 617472 | bytes 4939776 | tf_op jit(solution)/shard_map/pallas_call | solution.py:131
  3.6 3.1 %collective-permute-start.3 = (f32[201,8,128]{2,1,0:T(8,128)}, f32[201,8,128]{2,1,0:T(8,128)S(1)}, u32[]{:S(2)}, u32[]{:S(2)}) collective-permute-start(f32[201,8,128]{2,1,0:T(8,128)} %get-tuple-element.14.refs_0_.refs_1_), channel_id=1, source_target_pairs={{0,8},{2,10},{4,12},{6,14},{8,0},{10,2},{12,4},{14,6},{16,24},{18,... | collective-permute-start | bytes 2469896 | tf_op jit(solution)/shard_map/ppermute | solution.py:45
  6.7 0.7 collective-permute-start.4
  7.4 2.5 %collective-permute-start.13 = (f32[1,8,128]{2,1,0:T(8,128)}, f32[1,8,128]{2,1,0:T(8,128)S(1)}, u32[]{:S(2)}, u32[]{:S(2)}) collective-permute-start(f32[1,8,128]{2,1,0:T(8,128)} %get-tuple-element.13.refs_1_.refs_0_.plan), channel_id=1, source_target_pairs={{0,6},{2,4},{4,2},{6,0},{8,14},{10,12},{12,10},{14,8},{16,22},{18,... | collective-permute-start | bytes 12296 | tf_op jit(solution)/shard_map/ppermute | solution.py:45
  9.9 0.5 collective-permute-start.2
  10.5 0.5 collective-permute-start
  11.0 1.3 %collective-permute-done.13.refs_0_ = f32[1,8,128]{2,1,0:T(8,128)S(1)} collective-permute-done((f32[1,8,128]{2,1,0:T(8,128)}, f32[1,8,128]{2,1,0:T(8,128)S(1)}, u32[]{:S(2)}, u32[]{:S(2)}) %collective-permute-start.13) | collective-permute-done | bytes 4128 | tf_op jit(solution)/shard_map/ppermute | solution.py:45
  12.2 1.5 %collective-permute-start.9 = (f32[201,8,128]{2,1,0:T(8,128)}, f32[201,8,128]{2,1,0:T(8,128)S(1)}, u32[]{:S(2)}, u32[]{:S(2)}) collective-permute-start(f32[201,8,128]{2,1,0:T(8,128)} %get-tuple-element.15.refs_1_.refs_2_), channel_id=1, source_target_pairs={{0,4},{2,6},{4,0},{6,2},{8,12},{10,14},{12,8},{14,10},{16,20},{18,... | collective-permute-start | bytes 2469896 | tf_op jit(solution)/shard_map/ppermute | solution.py:45
  13.7 11.5 %collective-permute-done.3.refs_2_ = f32[201,8,128]{2,1,0:T(8,128)S(1)} collective-permute-done((f32[201,8,128]{2,1,0:T(8,128)}, f32[201,8,128]{2,1,0:T(8,128)S(1)}, u32[]{:S(2)}, u32[]{:S(2)}) %collective-permute-start.3) | collective-permute-done | bytes 823328 | tf_op jit(solution)/shard_map/ppermute | solution.py:45
  25.2 1.7 %collective-permute-start.5 = (f32[201,8,128]{2,1,0:T(8,128)}, f32[201,8,128]{2,1,0:T(8,128)}, u32[]{:S(2)}, u32[]{:S(2)}) collective-permute-start(f32[201,8,128]{2,1,0:T(8,128)} %get-tuple-element.16.refs_2_), channel_id=1, source_target_pairs={{0,8},{2,10},{4,12},{6,14},{8,0},{10,2},{12,4},{14,6},{16,24},{18,... | collective-permute-start | bytes 2469896 | tf_op jit(solution)/shard_map/ppermute | solution.py:45
  27.0 0.0 collective-permute-done.4.refs_3_
  27.0 1.6 %collective-permute-start.6 = (f32[201,8,128]{2,1,0:T(8,128)}, f32[201,8,128]{2,1,0:T(8,128)}, u32[]{:S(2)}, u32[]{:S(2)}) collective-permute-start(f32[201,8,128]{2,1,0:T(8,128)} %get-tuple-element.16.refs_2_), channel_id=1, source_target_pairs={{8,16},{10,18},{12,20},{14,22},{16,8},{18,10},{20,12},{22,14},{9,1... | collective-permute-start | bytes 2469896 | tf_op jit(solution)/shard_map/ppermute | solution.py:45
  28.5 1.1 collective-permute-done.2.refs_0_.refs_3_.refs_2_
  29.7 0.5 collective-permute-start.8
  30.2 1.8 %collective-permute-done.refs_1_.refs_3_ = f32[201,8,128]{2,1,0:T(8,128)} collective-permute-done((f32[201,8,128]{2,1,0:T(8,128)}, f32[201,8,128]{2,1,0:T(8,128)}, u32[]{:S(2)}, u32[]{:S(2)}) %collective-permute-start) | collective-permute-done | bytes 823328 | tf_op jit(solution)/shard_map/ppermute | solution.py:45
  32.0 7.2 %collective-permute-start.1 = (f32[201,8,128]{2,1,0:T(8,128)}, f32[201,8,128]{2,1,0:T(8,128)}, u32[]{:S(2)}, u32[]{:S(2)}) collective-permute-start(f32[201,8,128]{2,1,0:T(8,128)} %collective-permute-done.refs_1_.refs_3_), channel_id=1, source_target_pairs={{0,8},{2,10},{8,16},{10,18},{12,4},{14,6},{16,24},{18,26},{20,12},... | collective-permute-start | bytes 2469896 | tf_op jit(solution)/shard_map/ppermute | solution.py:45
  39.2 2.5 %shard_map.76 = f32[200,8,128]{2,1,0:T(8,128)} custom-call(f32[1,8,128]{2,1,0:T(8,128)S(1)} %collective-permute-done.13.refs_0_, f32[201,8,128]{2,1,0:T(8,128)} %get-tuple-element.14.refs_0_.refs_1_, f32[201,8,128]{2,1,0:T(8,128)S(1)} %collective-permute-done.3.refs_2_, f32[201,8,128]{2,1,0:T(8,128)S(1)} %collective-permute-done.4.refs_3_), custom_call_target="tpu_custom_call" | custom-call | flops 1638400 | bytes 3276800 | tf_op jit(solution)/shard_map/pallas_call | solution.py:259
  41.7 7.9 %collective-permute-done.9.refs_4_ = f32[201,8,128]{2,1,0:T(8,128)S(1)} collective-permute-done((f32[201,8,128]{2,1,0:T(8,128)}, f32[201,8,128]{2,1,0:T(8,128)S(1)}, u32[]{:S(2)}, u32[]{:S(2)}) %collective-permute-start.9) | collective-permute-done | bytes 823328 | tf_op jit(solution)/shard_map/ppermute | solution.py:45
  49.5 0.9 copy-done
  50.4 1.5 %collective-permute-start.14 = (f32[200,8,128]{2,1,0:T(8,128)}, f32[200,8,128]{2,1,0:T(8,128)}, u32[]{:S(2)}, u32[]{:S(2)}) collective-permute-start(f32[200,8,128]{2,1,0:T(8,128)} %shard_map.76), channel_id=1, source_target_pairs={{0,2},{2,0},{4,6},{6,4},{8,10},{10,8},{12,14},{14,12},{16,18},{18,... | collective-permute-start | bytes 2457608 | tf_op jit(solution)/shard_map/ppermute | solution.py:45
  51.9 2.5 %shard_map.65 = f32[32,1,128]{2,1,0:T(1,128)} custom-call(f32[201,8,128]{2,1,0:T(8,128)} %get-tuple-element.14.refs_0_.refs_1_, f32[201,8,128]{2,1,0:T(8,128)} %get-tuple-element.15.refs_1_.refs_2_, f32[201,8,128]{2,1,0:T(8,128)} %get-tuple-element.16.refs_2_), custom_call_target="tpu_custom_call" | custom-call | flops 617472 | bytes 3293184 | tf_op jit(solution)/shard_map/pallas_call | solution.py:169
  54.4 4.7 %all-to-all-start = ((f32[32,1,128]{2,1,0:T(1,128)}), f32[32,1,128]{2,1,0:T(1,128)S(1)}, u32[]{:S(2)}, u32[]{:S(2)}) async-start(f32[32,1,128]{2,1,0:T(1,128)} %shard_map.65), calls=%async_computation | async-start | bytes 32768 | tf_op jit(solution)/shard_map/all_to_all | solution.py:177
  59.2 11.5 %all-to-all-done = f32[32,1,128]{2,1,0:T(1,128)S(1)} async-done(((f32[32,1,128]{2,1,0:T(1,128)}), f32[32,1,128]{2,1,0:T(1,128)S(1)}, u32[]{:S(2)}, u32[]{:S(2)}) %all-to-all-start) | async-done | bytes 16416 | tf_op jit(solution)/shard_map/all_to_all | solution.py:177
  70.7 0.1 fusion.19
  70.8 0.1 reshape_squeeze.8
  70.9 0.1 reshape_squeeze.7
  71.0 0.1 convert_element_type.42
  71.1 0.1 slice_reduce_fusion
  71.2 0.1 reshape.161
  71.3 0.7 shard_map.66.refs_0_
  72.0 0.0 copy-start.1
  72.0 0.0 copy-start.2
  72.0 1.8 %shard_map.74 = f32[200,8,128]{2,1,0:T(8,128)S(1)} custom-call(f32[4,8,128]{2,1,0:T(8,128)S(1)} %shard_map.66.refs_0_, f32[201,8,128]{2,1,0:T(8,128)} %get-tuple-element.14.refs_0_.refs_1_, f32[201,8,128]{2,1,0:T(8,128)S(1)} %collective-permute-done.3.refs_2_, f32[201,8,128]{2,1,0:T(8,128)S(1)} %collective-permute-done.4.refs_3_), custom_call_target="tpu_custom_call" | custom-call | flops 1638400 | bytes 3276800 | tf_op jit(solution)/shard_map/pallas_call | solution.py:259
  73.8 1.8 %shard_map.72 = f32[200,8,128]{2,1,0:T(8,128)S(1)} custom-call(f32[4,8,128]{2,1,0:T(8,128)S(1)} %shard_map.66.refs_0_, f32[201,8,128]{2,1,0:T(8,128)} %get-tuple-element.15.refs_1_.refs_2_, f32[201,8,128]{2,1,0:T(8,128)S(1)} %collective-permute-done.2.refs_0_.refs_3_.refs_2_), custom_call_target="tpu_custom_call" | custom-call | flops 1638400 | bytes 2457600 | tf_op jit(solution)/shard_map/pallas_call | solution.py:259
  75.6 0.0 copy-done.1
  75.6 2.3 %shard_map.70 = (f32[200,8,128]{2,1,0:T(8,128)S(1)}, f32[200,8,128]{2,1,0:T(8,128)S(1)}) custom-call(f32[4,8,128]{2,1,0:T(8,128)S(1)} %shard_map.66.refs_0_, f32[1,8,128]{2,1,0:T(8,128)S(1)} %copy-done.2, f32[201,8,128]{2,1,0:T(8,128)} %get-tuple-element.15.refs_1_.refs_2_, f32[201,8,128]{2,1,0:T(8,128)S(1)} %collective-permute-done.2.refs_0_.refs_3_.refs_2_, ...), custom_call_target="tpu_custom_call" | custom-call | flops 3276800 | bytes 4096000 | tf_op jit(solution)/shard_map/pallas_call | solution.py:259
  78.0 0.0 collective-permute-done.5.refs_4_
  78.0 0.4 collective-permute-start.12
  78.4 0.0 collective-permute-done.6.refs_5_
  78.4 1.3 %collective-permute-start.10 = (f32[200,8,128]{2,1,0:T(8,128)S(1)}, f32[200,8,128]{2,1,0:T(8,128)S(1)}, u32[]{:S(2)}, u32[]{:S(2)}) collective-permute-start(f32[200,8,128]{2,1,0:T(8,128)S(1)} %shard_map.72), channel_id=1, source_target_pairs={{4,12},{6,14},{8,0},{10,2},{12,20},{14,22},{16,8},{18,10},{20,28},... | collective-permute-start | bytes 2457608 | tf_op jit(solution)/shard_map/ppermute | solution.py:45
  79.7 3.2 %shard_map.67 = (f32[200,8,128]{2,1,0:T(8,128)S(1)}, f32[200,8,128]{2,1,0:T(8,128)S(1)}) custom-call(f32[4,8,128]{2,1,0:T(8,128)S(1)} %shard_map.66.refs_0_, f32[1,8,128]{2,1,0:T(8,128)S(1)} %copy-done.2, f32[201,8,128]{2,1,0:T(8,128)} %get-tuple-element.16.refs_2_, f32[201,8,128]{2,1,0:T(8,128)} %collective-permute-done.refs_1_.refs_3_, ...), custom_call_target="tpu_custom_call" | custom-call | flops 3276800 | bytes 4915200 | tf_op jit(solution)/shard_map/pallas_call | solution.py:259
  82.9 0.0 collective-permute-done.14.refs_4_
  82.9 1.9 %shard_map.77 = f32[200,8,128]{2,1,0:T(8,128)S(1)} custom-call(f32[4,8,128]{2,1,0:T(8,128)S(1)} %shard_map.66.refs_0_, f32[201,8,128]{2,1,0:T(8,128)} %get-tuple-element.14.refs_0_.refs_1_, f32[201,8,128]{2,1,0:T(8,128)S(1)} %collective-permute-done.3.refs_2_, f32[201,8,128]{2,1,0:T(8,128)S(1)} %collective-permute-done.4.refs_3_, ...), custom_call_target="tpu_custom_call" | custom-call | flops 1638400 | bytes 4096000 | tf_op jit(solution)/shard_map/pallas_call | solution.py:259
  84.8 3.1 %collective-permute-start.15 = (f32[200,8,128]{2,1,0:T(8,128)S(1)}, f32[200,8,128]{2,1,0:T(8,128)S(1)}, u32[]{:S(2)}, u32[]{:S(2)}) collective-permute-start(f32[200,8,128]{2,1,0:T(8,128)S(1)} %shard_map.77), channel_id=1, source_target_pairs={{0,4},{2,6},{4,0},{6,2},{8,12},{10,14},{12,8},{14,10},{16,20},{18,... | collective-permute-start | bytes 2457608 | tf_op jit(solution)/shard_map/ppermute | solution.py:45
  87.9 0.0 collective-permute-done.8.refs_1_
  87.9 1.3 %shard_map.73 = f32[200,8,128]{2,1,0:T(8,128)S(1)} custom-call(f32[4,8,128]{2,1,0:T(8,128)S(1)} %shard_map.66.refs_0_, f32[201,8,128]{2,1,0:T(8,128)S(1)} %collective-permute-done.8.refs_1_, f32[200,8,128]{2,1,0:T(8,128)S(1)} %get-tuple-element.20.refs_2_), custom_call_target="tpu_custom_call" | custom-call | flops 1638400 | bytes 2457600 | tf_op jit(solution)/shard_map/pallas_call | solution.py:259
  89.2 2.5 %collective-permute-start.11 = (f32[200,8,128]{2,1,0:T(8,128)S(1)}, f32[200,8,128]{2,1,0:T(8,128)S(1)}, u32[]{:S(2)}, u32[]{:S(2)}) collective-permute-start(f32[200,8,128]{2,1,0:T(8,128)S(1)} %shard_map.73), channel_id=1, source_target_pairs={{0,8},{2,10},{8,16},{10,18},{12,4},{14,6},{16,24},{18,26},{20,12},... | collective-permute-start | bytes 2457608 | tf_op jit(solution)/shard_map/ppermute | solution.py:45
  91.7 0.0 collective-permute-done.1.refs_1_
  91.7 1.4 %shard_map.69 = f32[200,8,128]{2,1,0:T(8,128)S(1)} custom-call(f32[4,8,128]{2,1,0:T(8,128)S(1)} %shard_map.66.refs_0_, f32[201,8,128]{2,1,0:T(8,128)} %collective-permute-done.1.refs_1_, f32[200,8,128]{2,1,0:T(8,128)S(1)} %get-tuple-element.18.refs_2_), custom_call_target="tpu_custom_call" | custom-call | flops 1638400 | bytes 2457600 | tf_op jit(solution)/shard_map/pallas_call | solution.py:259
  93.2 0.4 collective-permute-start.7
  93.6 0.3 add_reduce_fusion
  93.9 0.1 multiply_reduce_fusion
  94.0 5.2 %collective-permute-done.12.refs_4_ = f32[200,8,128]{2,1,0:T(8,128)S(1)} collective-permute-done((f32[200,8,128]{2,1,0:T(8,128)S(1)}, f32[200,8,128]{2,1,0:T(8,128)S(1)}, u32[]{:S(2)}, u32[]{:S(2)}) %collective-permute-start.12) | collective-permute-done | bytes 819232 | tf_op jit(solution)/shard_map/ppermute | solution.py:45
  99.2 1.6 %shard_map.75.refs_0_ = f32[200,8,128]{2,1,0:T(8,128)S(1)} custom-call(f32[1,8,128]{2,1,0:T(8,128)S(1)} %copy-done.2, f32[201,8,128]{2,1,0:T(8,128)} %get-tuple-element.14.refs_0_.refs_1_, f32[201,8,128]{2,1,0:T(8,128)S(1)} %collective-permute-done.3.refs_2_, f32[201,8,128]{2,1,0:T(8,128)S(1)} %collective-permute-done.4.refs_3_, ...), custom_call_target="tpu_custom_call" | custom-call | flops 1638400 | bytes 4096000 | tf_op jit(solution)/shard_map/pallas_call | solution.py:259
  100.8 0.0 copy-start.3
  100.8 0.9 shard_map.71.refs_0_
  101.7 1.4 %shard_map.68.refs_0_ = f32[200,8,128]{2,1,0:T(8,128)S(1)} custom-call(f32[1,8,128]{2,1,0:T(8,128)S(1)} %copy-done.2, f32[201,8,128]{2,1,0:T(8,128)} %collective-permute-done.1.refs_1_, f32[200,8,128]{2,1,0:T(8,128)S(1)} %get-tuple-element.17.refs_2_), custom_call_target="tpu_custom_call" | custom-call | flops 1638400 | bytes 2457600 | tf_op jit(solution)/shard_map/pallas_call | solution.py:259
  103.1 2.4 %collective-permute-done.15.refs_1_ = f32[200,8,128]{2,1,0:T(8,128)S(1)} collective-permute-done((f32[200,8,128]{2,1,0:T(8,128)S(1)}, f32[200,8,128]{2,1,0:T(8,128)S(1)}, u32[]{:S(2)}, u32[]{:S(2)}) %collective-permute-start.15) | collective-permute-done | bytes 819232 | tf_op jit(solution)/shard_map/ppermute | solution.py:45
  105.6 3.0 %shard_map.78.refs_3_ = f32[10,3,8,2560]{3,2,1,0:T(8,128)} custom-call(f32[1,8,128]{2,1,0:T(8,128)S(1)} %copy-done.2, s32[10]{0:T(128)S(1)} %copy-done.3, f32[3]{0:T(128)S(1)} %div.13.ratio, f32[200,8,128]{2,1,0:T(8,128)S(1)} %shard_map.75.refs_0_, f32[200,8,128]{2,1,0:T(8,128)S(1)} %collective-permute-done.15.refs_1_), custom_call_target="tpu_custom_call" | custom-call | flops 12288000 | bytes 2457600 | tf_op jit(solution)/shard_map/pallas_call | solution.py:352
  108.6 0.0 collective-permute-done.10.refs_1_
  108.6 0.0 collective-permute-done.11.refs_2_
  108.6 3.5 %shard_map.79.refs_2_ = f32[10,3,8,2560]{3,2,1,0:T(8,128)} custom-call(f32[1,8,128]{2,1,0:T(8,128)S(1)} %copy-done.2, s32[10]{0:T(128)S(1)} %copy-done.3, f32[3]{0:T(128)S(1)} %div.13.ratio, f32[200,8,128]{2,1,0:T(8,128)S(1)} %shard_map.71.refs_0_, f32[200,8,128]{2,1,0:T(8,128)S(1)} %collective-permute-done.10.refs_1_, ...), custom_call_target="tpu_custom_call", output_to_operand_aliasing={{}: (6, {})} | custom-call | flops 12288000 | bytes 3276800 | tf_op jit(solution)/shard_map/pallas_call | solution.py:352
  112.1 3.4 %collective-permute-done.7.refs_1_ = f32[200,8,128]{2,1,0:T(8,128)S(1)} collective-permute-done((f32[200,8,128]{2,1,0:T(8,128)S(1)}, f32[200,8,128]{2,1,0:T(8,128)S(1)}, u32[]{:S(2)}, u32[]{:S(2)}) %collective-permute-start.7) | collective-permute-done | bytes 819232 | tf_op jit(solution)/shard_map/ppermute | solution.py:45
  115.5 3.0 %shard_map.80 = f32[10,3,8,2560]{3,2,1,0:T(8,128)} custom-call(f32[1,8,128]{2,1,0:T(8,128)S(1)} %copy-done.2, s32[10]{0:T(128)S(1)} %copy-done.3, f32[3]{0:T(128)S(1)} %div.13.ratio, f32[200,8,128]{2,1,0:T(8,128)S(1)} %shard_map.68.refs_0_, f32[200,8,128]{2,1,0:T(8,128)S(1)} %collective-permute-done.7.refs_1_, ...), custom_call_target="tpu_custom_call", output_to_operand_aliasing={{}: (5, {})} | custom-call | flops 12288000 | bytes 2457600 | tf_op jit(solution)/shard_map/pallas_call | solution.py:352
  (9 shorter events, 0.1 us)
Async XLA Ops:
  3.6 21.7 %collective-permute-start.3 = (f32[201,8,128]{2,1,0:T(8,128)}, f32[201,8,128]{2,1,0:T(8,128)S(1)}, u32[]{:S(2)}, u32[]{:S(2)}) collective-permute-start(f32[201,8,128]{2,1,0:T(8,128)} %get-tuple-element.14.refs_0_.refs_1_), channel_id=1, source_target_pairs={{0,8},{2,10},{4,12},{6,14},{8,0},{10,2},{12,4},{14,6},{16,24},{18,... | collective-permute-start | bytes 2469896 | tf_op jit(solution)/shard_map/ppermute | solution.py:45
  6.7 20.3 %collective-permute-start.4 = (f32[201,8,128]{2,1,0:T(8,128)}, f32[201,8,128]{2,1,0:T(8,128)S(1)}, u32[]{:S(2)}, u32[]{:S(2)}) collective-permute-start(f32[201,8,128]{2,1,0:T(8,128)} %get-tuple-element.14.refs_0_.refs_1_), channel_id=1, source_target_pairs={{8,16},{10,18},{12,20},{14,22},{16,8},{18,10},{20,12},{22,14},{9,1... | collective-permute-start | bytes 2469896 | tf_op jit(solution)/shard_map/ppermute | solution.py:45
  7.4 4.8 %collective-permute-start.13 = (f32[1,8,128]{2,1,0:T(8,128)}, f32[1,8,128]{2,1,0:T(8,128)S(1)}, u32[]{:S(2)}, u32[]{:S(2)}) collective-permute-start(f32[1,8,128]{2,1,0:T(8,128)} %get-tuple-element.13.refs_1_.refs_0_.plan), channel_id=1, source_target_pairs={{0,6},{2,4},{4,2},{6,0},{8,14},{10,12},{12,10},{14,8},{16,22},{18,... | collective-permute-start | bytes 12296 | tf_op jit(solution)/shard_map/ppermute | solution.py:45
  9.9 19.8 %collective-permute-start.2 = (f32[201,8,128]{2,1,0:T(8,128)}, f32[201,8,128]{2,1,0:T(8,128)S(1)}, u32[]{:S(2)}, u32[]{:S(2)}) collective-permute-start(f32[201,8,128]{2,1,0:T(8,128)} %get-tuple-element.15.refs_1_.refs_2_), channel_id=1, source_target_pairs={{0,2},{2,0},{4,6},{6,4},{8,10},{10,8},{12,14},{14,12},{16,18},{18,... | collective-permute-start | bytes 2469896 | tf_op jit(solution)/shard_map/ppermute | solution.py:45
  10.5 21.5 %collective-permute-start = (f32[201,8,128]{2,1,0:T(8,128)}, f32[201,8,128]{2,1,0:T(8,128)}, u32[]{:S(2)}, u32[]{:S(2)}) collective-permute-start(f32[201,8,128]{2,1,0:T(8,128)} %get-tuple-element.16.refs_2_), channel_id=1, source_target_pairs={{0,4},{2,6},{4,0},{6,2},{8,12},{10,14},{12,8},{14,10},{16,20},{18,... | collective-permute-start | bytes 2469896 | tf_op jit(solution)/shard_map/ppermute | solution.py:45
  12.2 37.3 %collective-permute-start.9 = (f32[201,8,128]{2,1,0:T(8,128)}, f32[201,8,128]{2,1,0:T(8,128)S(1)}, u32[]{:S(2)}, u32[]{:S(2)}) collective-permute-start(f32[201,8,128]{2,1,0:T(8,128)} %get-tuple-element.15.refs_1_.refs_2_), channel_id=1, source_target_pairs={{0,4},{2,6},{4,0},{6,2},{8,12},{10,14},{12,8},{14,10},{16,20},{18,... | collective-permute-start | bytes 2469896 | tf_op jit(solution)/shard_map/ppermute | solution.py:45
  25.2 52.7 %collective-permute-start.5 = (f32[201,8,128]{2,1,0:T(8,128)}, f32[201,8,128]{2,1,0:T(8,128)}, u32[]{:S(2)}, u32[]{:S(2)}) collective-permute-start(f32[201,8,128]{2,1,0:T(8,128)} %get-tuple-element.16.refs_2_), channel_id=1, source_target_pairs={{0,8},{2,10},{4,12},{6,14},{8,0},{10,2},{12,4},{14,6},{16,24},{18,... | collective-permute-start | bytes 2469896 | tf_op jit(solution)/shard_map/ppermute | solution.py:45
  27.0 51.4 %collective-permute-start.6 = (f32[201,8,128]{2,1,0:T(8,128)}, f32[201,8,128]{2,1,0:T(8,128)}, u32[]{:S(2)}, u32[]{:S(2)}) collective-permute-start(f32[201,8,128]{2,1,0:T(8,128)} %get-tuple-element.16.refs_2_), channel_id=1, source_target_pairs={{8,16},{10,18},{12,20},{14,22},{16,8},{18,10},{20,12},{22,14},{9,1... | collective-permute-start | bytes 2469896 | tf_op jit(solution)/shard_map/ppermute | solution.py:45
  29.7 58.2 %collective-permute-start.8 = (f32[201,8,128]{2,1,0:T(8,128)S(1)}, f32[201,8,128]{2,1,0:T(8,128)S(1)}, u32[]{:S(2)}, u32[]{:S(2)}) collective-permute-start(f32[201,8,128]{2,1,0:T(8,128)S(1)} %collective-permute-done.2.refs_0_.refs_3_.refs_2_), channel_id=1, source_target_pairs={{0,4},{2,6},{4,0},{6,2},{8,12},{10,14},{12,8},{14,10},{16,20},{18,... | collective-permute-start | bytes 2469896 | tf_op jit(solution)/shard_map/ppermute | solution.py:45
  32.0 59.8 %collective-permute-start.1 = (f32[201,8,128]{2,1,0:T(8,128)}, f32[201,8,128]{2,1,0:T(8,128)}, u32[]{:S(2)}, u32[]{:S(2)}) collective-permute-start(f32[201,8,128]{2,1,0:T(8,128)} %collective-permute-done.refs_1_.refs_3_), channel_id=1, source_target_pairs={{0,8},{2,10},{8,16},{10,18},{12,4},{14,6},{16,24},{18,26},{20,12},... | collective-permute-start | bytes 2469896 | tf_op jit(solution)/shard_map/ppermute | solution.py:45
  49.5 0.9 copy-start
  50.4 32.5 %collective-permute-start.14 = (f32[200,8,128]{2,1,0:T(8,128)}, f32[200,8,128]{2,1,0:T(8,128)}, u32[]{:S(2)}, u32[]{:S(2)}) collective-permute-start(f32[200,8,128]{2,1,0:T(8,128)} %shard_map.76), channel_id=1, source_target_pairs={{0,2},{2,0},{4,6},{6,4},{8,10},{10,8},{12,14},{14,12},{16,18},{18,... | collective-permute-start | bytes 2457608 | tf_op jit(solution)/shard_map/ppermute | solution.py:45
  54.4 16.3 %all-to-all-start = ((f32[32,1,128]{2,1,0:T(1,128)}), f32[32,1,128]{2,1,0:T(1,128)S(1)}, u32[]{:S(2)}, u32[]{:S(2)}) async-start(f32[32,1,128]{2,1,0:T(1,128)} %shard_map.65), calls=%async_computation | async-start | bytes 32768 | tf_op jit(solution)/shard_map/all_to_all | solution.py:177
  72.0 3.6 %copy-start.1 = (f32[201,8,128]{2,1,0:T(8,128)S(1)}, f32[201,8,128]{2,1,0:T(8,128)}, u32[]{:S(2)}) copy-start(f32[201,8,128]{2,1,0:T(8,128)} %copy-done) | copy-start | bytes 2469892
  72.0 3.6 %copy-start.2 = (f32[1,8,128]{2,1,0:T(8,128)S(1)}, f32[1,8,128]{2,1,0:T(8,128)}, u32[]{:S(2)}) copy-start(f32[1,8,128]{2,1,0:T(8,128)} %get-tuple-element.13.refs_1_.refs_0_.plan) | copy-start | bytes 12292
  78.0 21.2 %collective-permute-start.12 = (f32[200,8,128]{2,1,0:T(8,128)S(1)}, f32[200,8,128]{2,1,0:T(8,128)S(1)}, u32[]{:S(2)}, u32[]{:S(2)}) collective-permute-start(f32[200,8,128]{2,1,0:T(8,128)S(1)} %shard_map.74), channel_id=1, source_target_pairs={{0,2},{2,0},{4,6},{6,4},{8,10},{10,8},{12,14},{14,12},{16,18},{18,... | collective-permute-start | bytes 2457608 | tf_op jit(solution)/shard_map/ppermute | solution.py:45
  78.4 30.2 %collective-permute-start.10 = (f32[200,8,128]{2,1,0:T(8,128)S(1)}, f32[200,8,128]{2,1,0:T(8,128)S(1)}, u32[]{:S(2)}, u32[]{:S(2)}) collective-permute-start(f32[200,8,128]{2,1,0:T(8,128)S(1)} %shard_map.72), channel_id=1, source_target_pairs={{4,12},{6,14},{8,0},{10,2},{12,20},{14,22},{16,8},{18,10},{20,28},... | collective-permute-start | bytes 2457608 | tf_op jit(solution)/shard_map/ppermute | solution.py:45
  84.8 20.7 %collective-permute-start.15 = (f32[200,8,128]{2,1,0:T(8,128)S(1)}, f32[200,8,128]{2,1,0:T(8,128)S(1)}, u32[]{:S(2)}, u32[]{:S(2)}) collective-permute-start(f32[200,8,128]{2,1,0:T(8,128)S(1)} %shard_map.77), channel_id=1, source_target_pairs={{0,4},{2,6},{4,0},{6,2},{8,12},{10,14},{12,8},{14,10},{16,20},{18,... | collective-permute-start | bytes 2457608 | tf_op jit(solution)/shard_map/ppermute | solution.py:45
  89.2 19.4 %collective-permute-start.11 = (f32[200,8,128]{2,1,0:T(8,128)S(1)}, f32[200,8,128]{2,1,0:T(8,128)S(1)}, u32[]{:S(2)}, u32[]{:S(2)}) collective-permute-start(f32[200,8,128]{2,1,0:T(8,128)S(1)} %shard_map.73), channel_id=1, source_target_pairs={{0,8},{2,10},{8,16},{10,18},{12,4},{14,6},{16,24},{18,26},{20,12},... | collective-permute-start | bytes 2457608 | tf_op jit(solution)/shard_map/ppermute | solution.py:45
  93.2 22.3 %collective-permute-start.7 = (f32[200,8,128]{2,1,0:T(8,128)S(1)}, f32[200,8,128]{2,1,0:T(8,128)S(1)}, u32[]{:S(2)}, u32[]{:S(2)}) collective-permute-start(f32[200,8,128]{2,1,0:T(8,128)S(1)} %shard_map.69), channel_id=1, source_target_pairs={{0,2},{2,0},{4,6},{6,4},{8,10},{10,8},{12,14},{14,12},{16,18},{18,... | collective-permute-start | bytes 2457608 | tf_op jit(solution)/shard_map/ppermute | solution.py:45
  100.8 4.7 %copy-start.3 = (s32[10]{0:T(128)S(1)}, s32[10]{0:T(128)}, u32[]{:S(2)}) copy-start(s32[10]{0:T(128)} %shifts.5) | copy-start | bytes 124

commit v2 on v1

--- a/solution.py
+++ b/solution.py
@@ -11,7 +11,7 @@
 
 REACH = 4
 LANES = 128
-VMEM_LIMIT = 12 * 1024 * 1024
+VMEM_LIMIT = 28 * 1024 * 1024
 START_LIMIT = 60 * 1024 * 1024
 
 
@@ -76,19 +76,23 @@
     return pl.CostEstimate(flops=flops * size, bytes_accessed=4 * size * count, transcendentals=0)
 
 
-def start_kernel(departure_row, lat_fraction, lon_fraction, extents, fields, *refs):
+def start_kernel(chosen, departure_row, lat_fraction, lon_fraction, extents, fields, *refs):
     parts, plan = refs[:-11], refs[-11]
     departure_s, lat_s, lon_s, extents_s, held, ready, tile_s = refs[-10:-3]
     sems, in_sems, out_sems = refs[-3:]
-    row_count, field_count, lev_count, lon_count = fields.shape
+    row_count, _, lev_count, lon_count = fields.shape
+    field_count = len(chosen)
     tile_count = lon_count // LANES
     scalars = (departure_row, lat_fraction, lon_fraction, extents)
     copies = [
         pltpu.make_async_copy(source, target, sems.at[k])
         for k, (source, target) in enumerate(zip(scalars, (departure_s, lat_s, lon_s, extents_s)))
     ]
-    rows = [pltpu.make_async_copy(fields.at[r], held.at[r], in_sems.at[r]) for r in range(row_count)]
-    for copy in copies + rows:
+    rows = [
+        [pltpu.make_async_copy(fields.at[r, f], held.at[k, r], in_sems.at[k, r]) for k, f in enumerate(chosen)]
+        for r in range(row_count)
+    ]
+    for copy in sum(rows, copies):
         copy.start()
     for copy in copies:
         copy.wait()
@@ -109,12 +113,13 @@
     for f, part in enumerate(parts):
         ships.append(pltpu.make_async_copy(tile_s, part.at[row_count * tile_count], out_sems.at[f, row_count]))
     for r in range(row_count):
-        rows[r].wait()
+        for copy in rows[r]:
+            copy.wait()
         for ship in ships[-field_count:]:
             ship.start()
         for f, part in enumerate(parts):
             for n in range(tile_count):
-                ready[f, r * tile_count + n] = held[r, f, :, n * LANES : (n + 1) * LANES]
+                ready[f, r * tile_count + n] = held[f, r, :, n * LANES : (n + 1) * LANES]
             span = pl.ds(r * tile_count, tile_count)
             ships.append(pltpu.make_async_copy(ready.at[f, span], part.at[span], out_sems.at[f, r]))
     for ship in ships[-field_count:]:
@@ -123,13 +128,14 @@
         ship.wait()
 
 
-def start(departure_row, lat_fraction, lon_fraction, extents, fields):
-    row_count, field_count, lev_count, lon_count = fields.shape
+def start(chosen, departure_row, lat_fraction, lon_fraction, extents, fields):
+    row_count, _, lev_count, lon_count = fields.shape
+    field_count = len(chosen)
     tiles = row_count * lon_count // LANES
     part = jax.ShapeDtypeStruct((tiles + 1, lev_count, LANES), jnp.float32)
     plan = jax.ShapeDtypeStruct((1, lev_count, LANES), jnp.float32)
     return pl.pallas_call(
-        start_kernel,
+        functools.partial(start_kernel, chosen),
         out_shape=[part] * field_count + [plan],
         in_specs=[hbm()] * 5,
         out_specs=[hbm()] * field_count + [vmem()],
@@ -138,11 +144,11 @@
             pltpu.SMEM(lat_fraction.shape, jnp.float32),
             pltpu.SMEM(lon_fraction.shape, jnp.float32),
             pltpu.SMEM(extents.shape, jnp.int32),
-            pltpu.VMEM(fields.shape, jnp.float32),
+            pltpu.VMEM((field_count, row_count, lev_count, lon_count), jnp.float32),
             pltpu.VMEM((field_count, tiles, lev_count, LANES), jnp.float32),
             pltpu.VMEM((lev_count, LANES), jnp.float32),
             pltpu.SemaphoreType.DMA((4,)),
-            pltpu.SemaphoreType.DMA((row_count,)),
+            pltpu.SemaphoreType.DMA((field_count, row_count)),
             pltpu.SemaphoreType.DMA((field_count, row_count + 1)),
         ],
         compiler_params=pltpu.CompilerParams(vmem_limit_bytes=START_LIMIT),
@@ -229,8 +235,9 @@
 def combine_kernel(row_count, jobs, *refs):
     me = lax.axis_index("lat")
     outs = refs[len(refs) - len(jobs) :]
-    for (bands, places, plan, line, seed), out in zip(jobs, outs):
-        out[...] = jnp.zeros_like(out) if seed is None else refs[seed][pl.ds(0, out.shape[0])]
+    for (bands, places, plan, line, seeds), out in zip(jobs, outs):
+        span = pl.ds(0, out.shape[0])
+        out[...] = sum((refs[seed][span] for seed in seeds[1:]), refs[seeds[0]][span]) if seeds else jnp.zeros_like(out)
         band_ids = [place(me) for place in places]
         add_bands(refs[plan].at[line(me)], [refs[b] for b in bands], band_ids, row_count, out)
 
@@ -246,13 +253,13 @@
         return len(known) - 1
 
     kept = []
-    for bands, places, (plan, line), *seed in jobs:
+    for bands, places, (plan, line), *seeds in jobs:
         held = [index(b, arrays) for b in bands]
-        kept.append((held, places, index(plan, scalars), line, index(seed[0], arrays) if seed else None))
+        kept.append((held, places, index(plan, scalars), line, [index(x, arrays) for x in seeds]))
     shift = len(scalars)
     kept = [
-        ([b + shift for b in held], places, plan, line, None if seed is None else seed + shift)
-        for held, places, plan, line, seed in kept
+        ([b + shift for b in held], places, plan, line, [x + shift for x in seeds])
+        for held, places, plan, line, seeds in kept
     ]
     tiles, lev_count, _ = jobs[0][0][0].shape
     outs = [jax.ShapeDtypeStruct((tiles - 1, lev_count, LANES), jnp.float32)] * len(jobs)
@@ -344,7 +351,7 @@
 def finish(plan, shifts, ratio, pieces, out_shape, out=None):
     row_count, _, lev_count, lon_count = out_shape
     given = [] if out is None else [out]
-    group = next(g for g in (5, 4, 3, 2, 1) if row_count % g == 0)
+    group = row_count
     flat, split = [], []
     for field, parts in pieces.items():
         split.append((field, tuple(range(len(flat), len(flat) + len(parts)))))
@@ -397,7 +404,9 @@
     near, middle, both = flip(1), flip(2), flip(3)
     even, odd = flip(REACH), across
     join = functools.partial(combine, row_count)
-    f0, f1, f2, plan = start(departure_row, lat_fraction, lon_fraction, extents, fields)
+    scalars = departure_row, lat_fraction, lon_fraction, extents
+    f2, f0, plan = start((2, 0), *scalars, fields)
+    f1, _ = start((1,), *scalars, fields)
     both_plan = send(plan, both)
     f2_middle = send(f2, middle)
     f0_even = send(f0, even)
@@ -436,11 +445,11 @@
     (f2_for_near,) = join(([f2_side], [side], near_plan, f2_early))
     f2_from_near = send(f2_for_near, near)
     (f0_own,) = join((*f0_all, own_plan, f0_from_near))
-    (f1_own,) = join(([f1_both], [both], own_plan, f1_own))
+    (f1_own,) = join(([f1_both], [both], own_plan, f1_own, f1_from_onward))
     (f2_own,) = join(([f2_side], [side], own_plan, f2_own))
 
     ratio = mass_ratio(table, row_count, field_count)
-    pieces = [f0_own, f0_from_middle], [f1_own, f1_from_onward, f1_from_back], [f2_own, f2_from_near]
+    pieces = [f0_own, f0_from_middle], [f1_own, f1_from_back], [f2_own, f2_from_near]
     out = None
     for field, parts in enumerate(pieces):
         out = finish(plan, lon_shift, ratio, {field: parts}, fields.shape, out)

time: 119 us -> 119 us (level)
  waiting for transfers between devices: 46 us -> 41.8 us
  starting transfers between devices: 33.7 us -> 36.3 us
    all_to_all x1, waiting for transfers between devices: 11.5 us -> 8.75 us  [exchange(): return lax.all_to_all(mine, ('lat', 'lev'), 0, 0, tiled=True)]
    ppermute x16, starting transfers between devices: 29 us -> 31.6 us  [send(): return lax.ppermute(block, 'lat', route)]
    pallas_call x1 -> x2, Pallas kernels: 3.57 us -> 5.89 us  [start(): pl.pallas_call(functools.partial(start_kernel, chosen), out_shape=[part]...]
    pallas_call x3, Pallas kernels: 9.58 us -> 8.1 us  [finish(): pl.pallas_call(functools.partial(finish_kernel, split), out_shape=jax.Sha...]
    ppermute x16, waiting for transfers between devices: 34.5 us -> 33.1 us  [send(): return lax.ppermute(block, 'lat', route)]
  transfers between devices with their start and end apart: 17 -> 17, of which waited for: 9 -> 10; matrix products, arithmetic and copies ran while one was open for 1% -> 1% of each run, Pallas kernels for 25% -> 27%
where the time goes in v2:
time: 119 us; the launch traced here: 118 us
  waiting for transfers between devices  41.8 us (35%)
  Pallas kernels  37.4 us (31%)
  starting transfers between devices  36.3 us (31%)
  local copies, waits for them, and re-layouts  1.37 us (1%)
    ppermute x16, waiting for transfers between devices, send(): return lax.ppermute(block, 'lat', route)  33.1 us
    ppermute x16, starting transfers between devices, send(): return lax.ppermute(block, 'lat', route)  31.6 us
    pallas_call x11, Pallas kernels, combine(): pl.pallas_call(functools.partial(combine_kernel, row_count, kept), out_sh...  20.2 us
    all_to_all x1, waiting for transfers between devices, exchange(): return lax.all_to_all(mine, ('lat', 'lev'), 0, 0, tiled=True)  8.75 us
    pallas_call x3, Pallas kernels, finish(): pl.pallas_call(functools.partial(finish_kernel, split), out_shape=jax.Sha...  8.1 us
    pallas_call x2, Pallas kernels, start(): pl.pallas_call(functools.partial(start_kernel, chosen), out_shape=[part]...  5.89 us
    all_to_all x1, starting transfers between devices, exchange(): return lax.all_to_all(mine, ('lat', 'lev'), 0, 0, tiled=True)  4.71 us
    pallas_call x1, Pallas kernels, exchange(): pl.pallas_call(functools.partial(sums_kernel, row_count), out_shape=jax.S...  2.49 us
  transfers between devices with their start and end apart: 17, of which 10 were waited for; matrix products, arithmetic and copies ran while one was open for 1% of the time, Pallas kernels for 27%

profile of v2, /device:TPU:0, one launch (start us, length us, event | category | flops | bytes accessed | tf_op | source)
XLA Modules:
  0.0 117.8 jit_solution(1877500200324422974)
XLA Ops:
  0.0 3.2 %shard_map.64 = (f32[201,8,128]{2,1,0:T(8,128)}, f32[201,8,128]{2,1,0:T(8,128)}, f32[1,8,128]{2,1,0:T(8,128)}) custom-call(s32[10]{0:T(128)} %departure_row.3, f32[10]{0:T(128)} %lat_fraction.3, f32[10]{0:T(128)} %lon_fraction.3, s32[1,2]{1,0:T(1,128)} %extents.3, f32[10,3,8,2560]{3,2,1,0:T(8,128)} %fields.3), custom_call_target="tpu_custom_call" | custom-call | flops 617472 | bytes 3293184 | tf_op jit(solution)/shard_map/pallas_call | solution.py:137
  3.2 3.1 %collective-permute-start.3 = (f32[201,8,128]{2,1,0:T(8,128)}, f32[201,8,128]{2,1,0:T(8,128)S(1)}, u32[]{:S(2)}, u32[]{:S(2)}) collective-permute-start(f32[201,8,128]{2,1,0:T(8,128)} %get-tuple-element.14.refs_0_.refs_1_), channel_id=1, source_target_pairs={{0,8},{2,10},{4,12},{6,14},{8,0},{10,2},{12,4},{14,6},{16,24},{18,... | collective-permute-start | bytes 2469896 | tf_op jit(solution)/shard_map/ppermute | solution.py:45
  6.3 0.7 collective-permute-start.4
  7.0 2.5 %collective-permute-start.13 = (f32[1,8,128]{2,1,0:T(8,128)}, f32[1,8,128]{2,1,0:T(8,128)S(1)}, u32[]{:S(2)}, u32[]{:S(2)}) collective-permute-start(f32[1,8,128]{2,1,0:T(8,128)} %get-tuple-element.13.refs_1_.refs_0_.plan), channel_id=1, source_target_pairs={{0,6},{2,4},{4,2},{6,0},{8,14},{10,12},{12,10},{14,8},{16,22},{18,... | collective-permute-start | bytes 12296 | tf_op jit(solution)/shard_map/ppermute | solution.py:45
  9.5 2.7 %shard_map.65 = (f32[201,8,128]{2,1,0:T(8,128)}, f32[1,8,128]{2,1,0:T(8,128)}) custom-call(s32[10]{0:T(128)} %departure_row.3, f32[10]{0:T(128)} %lat_fraction.3, f32[10]{0:T(128)} %lon_fraction.3, s32[1,2]{1,0:T(1,128)} %extents.3, f32[10,3,8,2560]{3,2,1,0:T(8,128)} %fields.3), custom_call_target="tpu_custom_call" | custom-call | flops 617472 | bytes 1646592 | tf_op jit(solution)/shard_map/pallas_call | solution.py:137
  12.2 0.6 collective-permute-start.2
  12.8 0.5 collective-permute-start
  13.4 0.0 collective-permute-done.13.refs_0_
  13.4 1.5 %collective-permute-start.9 = (f32[201,8,128]{2,1,0:T(8,128)}, f32[201,8,128]{2,1,0:T(8,128)S(1)}, u32[]{:S(2)}, u32[]{:S(2)}) collective-permute-start(f32[201,8,128]{2,1,0:T(8,128)} %get-tuple-element.15.refs_1_.refs_2_), channel_id=1, source_target_pairs={{0,4},{2,6},{4,0},{6,2},{8,12},{10,14},{12,8},{14,10},{16,20},{18,... | collective-permute-start | bytes 2469896 | tf_op jit(solution)/shard_map/ppermute | solution.py:45
  14.9 10.0 %collective-permute-done.3.refs_2_ = f32[201,8,128]{2,1,0:T(8,128)S(1)} collective-permute-done((f32[201,8,128]{2,1,0:T(8,128)}, f32[201,8,128]{2,1,0:T(8,128)S(1)}, u32[]{:S(2)}, u32[]{:S(2)}) %collective-permute-start.3) | collective-permute-done | bytes 823328 | tf_op jit(solution)/shard_map/ppermute | solution.py:45
  24.9 1.7 %collective-permute-start.5 = (f32[201,8,128]{2,1,0:T(8,128)}, f32[201,8,128]{2,1,0:T(8,128)}, u32[]{:S(2)}, u32[]{:S(2)}) collective-permute-start(f32[201,8,128]{2,1,0:T(8,128)} %get-tuple-element.16.refs_2_), channel_id=1, source_target_pairs={{0,8},{2,10},{4,12},{6,14},{8,0},{10,2},{12,4},{14,6},{16,24},{18,... | collective-permute-start | bytes 2469896 | tf_op jit(solution)/shard_map/ppermute | solution.py:45
  26.6 0.0 collective-permute-done.4.refs_3_
  26.6 1.6 %collective-permute-start.6 = (f32[201,8,128]{2,1,0:T(8,128)}, f32[201,8,128]{2,1,0:T(8,128)}, u32[]{:S(2)}, u32[]{:S(2)}) collective-permute-start(f32[201,8,128]{2,1,0:T(8,128)} %get-tuple-element.16.refs_2_), channel_id=1, source_target_pairs={{8,16},{10,18},{12,20},{14,22},{16,8},{18,10},{20,12},{22,14},{9,1... | collective-permute-start | bytes 2469896 | tf_op jit(solution)/shard_map/ppermute | solution.py:45
  28.2 3.9 %collective-permute-done.2.refs_0_.refs_3_.refs_2_ = f32[201,8,128]{2,1,0:T(8,128)S(1)} collective-permute-done((f32[201,8,128]{2,1,0:T(8,128)}, f32[201,8,128]{2,1,0:T(8,128)S(1)}, u32[]{:S(2)}, u32[]{:S(2)}) %collective-permute-start.2) | collective-permute-done | bytes 823328 | tf_op jit(solution)/shard_map/ppermute | solution.py:45
  32.0 0.5 collective-permute-start.8
  32.5 1.8 %collective-permute-done.refs_1_.refs_3_ = f32[201,8,128]{2,1,0:T(8,128)} collective-permute-done((f32[201,8,128]{2,1,0:T(8,128)}, f32[201,8,128]{2,1,0:T(8,128)}, u32[]{:S(2)}, u32[]{:S(2)}) %collective-permute-start) | collective-permute-done | bytes 823328 | tf_op jit(solution)/shard_map/ppermute | solution.py:45
  34.4 7.2 %collective-permute-start.1 = (f32[201,8,128]{2,1,0:T(8,128)}, f32[201,8,128]{2,1,0:T(8,128)}, u32[]{:S(2)}, u32[]{:S(2)}) collective-permute-start(f32[201,8,128]{2,1,0:T(8,128)} %collective-permute-done.refs_1_.refs_3_), channel_id=1, source_target_pairs={{0,8},{2,10},{8,16},{10,18},{12,4},{14,6},{16,24},{18,26},{20,12},... | collective-permute-start | bytes 2469896 | tf_op jit(solution)/shard_map/ppermute | solution.py:45
  41.5 2.5 %shard_map.77 = f32[200,8,128]{2,1,0:T(8,128)} custom-call(f32[1,8,128]{2,1,0:T(8,128)S(1)} %collective-permute-done.13.refs_0_, f32[201,8,128]{2,1,0:T(8,128)} %get-tuple-element.14.refs_0_.refs_1_, f32[201,8,128]{2,1,0:T(8,128)S(1)} %collective-permute-done.3.refs_2_, f32[201,8,128]{2,1,0:T(8,128)S(1)} %collective-permute-done.4.refs_3_), custom_call_target="tpu_custom_call" | custom-call | flops 1638400 | bytes 3276800 | tf_op jit(solution)/shard_map/pallas_call | solution.py:266
  44.0 7.9 %collective-permute-done.9.refs_4_ = f32[201,8,128]{2,1,0:T(8,128)S(1)} collective-permute-done((f32[201,8,128]{2,1,0:T(8,128)}, f32[201,8,128]{2,1,0:T(8,128)S(1)}, u32[]{:S(2)}, u32[]{:S(2)}) %collective-permute-start.9) | collective-permute-done | bytes 823328 | tf_op jit(solution)/shard_map/ppermute | solution.py:45
  51.9 0.9 copy-done
  52.8 1.5 %collective-permute-start.14 = (f32[200,8,128]{2,1,0:T(8,128)}, f32[200,8,128]{2,1,0:T(8,128)}, u32[]{:S(2)}, u32[]{:S(2)}) collective-permute-start(f32[200,8,128]{2,1,0:T(8,128)} %shard_map.77), channel_id=1, source_target_pairs={{0,2},{2,0},{4,6},{6,4},{8,10},{10,8},{12,14},{14,12},{16,18},{18,... | collective-permute-start | bytes 2457608 | tf_op jit(solution)/shard_map/ppermute | solution.py:45
  54.3 2.5 %shard_map.66 = f32[32,1,128]{2,1,0:T(1,128)} custom-call(f32[201,8,128]{2,1,0:T(8,128)} %get-tuple-element.14.refs_0_.refs_1_, f32[201,8,128]{2,1,0:T(8,128)} %get-tuple-element.15.refs_1_.refs_2_, f32[201,8,128]{2,1,0:T(8,128)} %get-tuple-element.16.refs_2_), custom_call_target="tpu_custom_call" | custom-call | flops 617472 | bytes 3293184 | tf_op jit(solution)/shard_map/pallas_call | solution.py:175
  56.8 4.7 %all-to-all-start = ((f32[32,1,128]{2,1,0:T(1,128)}), f32[32,1,128]{2,1,0:T(1,128)S(1)}, u32[]{:S(2)}, u32[]{:S(2)}) async-start(f32[32,1,128]{2,1,0:T(1,128)} %shard_map.66), calls=%async_computation | async-start | bytes 32768 | tf_op jit(solution)/shard_map/all_to_all | solution.py:183
  61.6 8.8 %all-to-all-done = f32[32,1,128]{2,1,0:T(1,128)S(1)} async-done(((f32[32,1,128]{2,1,0:T(1,128)}), f32[32,1,128]{2,1,0:T(1,128)S(1)}, u32[]{:S(2)}, u32[]{:S(2)}) %all-to-all-start) | async-done | bytes 16416 | tf_op jit(solution)/shard_map/all_to_all | solution.py:183
  70.3 0.1 fusion.19
  70.4 0.1 reshape_squeeze.8
  70.5 0.1 reshape_squeeze.7
  70.6 0.1 convert_element_type.42
  70.7 0.1 slice_reduce_fusion
  70.8 0.1 reshape.161
  70.9 0.7 shard_map.67.refs_0_
  71.6 0.0 copy-start.1
  71.6 0.0 copy-start.2
  71.7 1.8 %shard_map.75 = f32[200,8,128]{2,1,0:T(8,128)S(1)} custom-call(f32[4,8,128]{2,1,0:T(8,128)S(1)} %shard_map.67.refs_0_, f32[201,8,128]{2,1,0:T(8,128)} %get-tuple-element.14.refs_0_.refs_1_, f32[201,8,128]{2,1,0:T(8,128)S(1)} %collective-permute-done.3.refs_2_, f32[201,8,128]{2,1,0:T(8,128)S(1)} %collective-permute-done.4.refs_3_), custom_call_target="tpu_custom_call" | custom-call | flops 1638400 | bytes 3276800 | tf_op jit(solution)/shard_map/pallas_call | solution.py:266
  73.4 1.8 %shard_map.72 = f32[200,8,128]{2,1,0:T(8,128)S(1)} custom-call(f32[4,8,128]{2,1,0:T(8,128)S(1)} %shard_map.67.refs_0_, f32[201,8,128]{2,1,0:T(8,128)} %get-tuple-element.15.refs_1_.refs_2_, f32[201,8,128]{2,1,0:T(8,128)S(1)} %collective-permute-done.2.refs_0_.refs_3_.refs_2_), custom_call_target="tpu_custom_call" | custom-call | flops 1638400 | bytes 2457600 | tf_op jit(solution)/shard_map/pallas_call | solution.py:266
  75.2 2.3 %shard_map.71 = (f32[200,8,128]{2,1,0:T(8,128)S(1)}, f32[200,8,128]{2,1,0:T(8,128)S(1)}) custom-call(f32[4,8,128]{2,1,0:T(8,128)S(1)} %shard_map.67.refs_0_, f32[1,8,128]{2,1,0:T(8,128)S(1)} %copy-done.2, f32[201,8,128]{2,1,0:T(8,128)} %get-tuple-element.15.refs_1_.refs_2_, f32[201,8,128]{2,1,0:T(8,128)S(1)} %collective-permute-done.2.refs_0_.refs_3_.refs_2_, ...), custom_call_target="tpu_custom_call" | custom-call | flops 3276800 | bytes 4096000 | tf_op jit(solution)/shard_map/pallas_call | solution.py:266
  77.6 0.0 collective-permute-done.5.refs_4_
  77.6 0.6 collective-permute-start.12
  78.2 0.0 collective-permute-done.6.refs_5_
  78.2 1.3 %collective-permute-start.10 = (f32[200,8,128]{2,1,0:T(8,128)S(1)}, f32[200,8,128]{2,1,0:T(8,128)S(1)}, u32[]{:S(2)}, u32[]{:S(2)}) collective-permute-start(f32[200,8,128]{2,1,0:T(8,128)S(1)} %shard_map.72), channel_id=1, source_target_pairs={{4,12},{6,14},{8,0},{10,2},{12,20},{14,22},{16,8},{18,10},{20,28},... | collective-permute-start | bytes 2457608 | tf_op jit(solution)/shard_map/ppermute | solution.py:45
  79.5 3.2 %shard_map.68 = (f32[200,8,128]{2,1,0:T(8,128)S(1)}, f32[200,8,128]{2,1,0:T(8,128)S(1)}) custom-call(f32[4,8,128]{2,1,0:T(8,128)S(1)} %shard_map.67.refs_0_, f32[1,8,128]{2,1,0:T(8,128)S(1)} %copy-done.2, f32[201,8,128]{2,1,0:T(8,128)} %get-tuple-element.16.refs_2_, f32[201,8,128]{2,1,0:T(8,128)} %collective-permute-done.refs_1_.refs_3_, ...), custom_call_target="tpu_custom_call" | custom-call | flops 3276800 | bytes 4915200 | tf_op jit(solution)/shard_map/pallas_call | solution.py:266
  82.7 0.0 collective-permute-done.14.refs_4_
  82.7 1.9 %shard_map.78 = f32[200,8,128]{2,1,0:T(8,128)S(1)} custom-call(f32[4,8,128]{2,1,0:T(8,128)S(1)} %shard_map.67.refs_0_, f32[201,8,128]{2,1,0:T(8,128)} %get-tuple-element.14.refs_0_.refs_1_, f32[201,8,128]{2,1,0:T(8,128)S(1)} %collective-permute-done.3.refs_2_, f32[201,8,128]{2,1,0:T(8,128)S(1)} %collective-permute-done.4.refs_3_, ...), custom_call_target="tpu_custom_call" | custom-call | flops 1638400 | bytes 4096000 | tf_op jit(solution)/shard_map/pallas_call | solution.py:266
  84.7 5.5 %collective-permute-start.15 = (f32[200,8,128]{2,1,0:T(8,128)S(1)}, f32[200,8,128]{2,1,0:T(8,128)S(1)}, u32[]{:S(2)}, u32[]{:S(2)}) collective-permute-start(f32[200,8,128]{2,1,0:T(8,128)S(1)} %shard_map.78), channel_id=1, source_target_pairs={{0,4},{2,6},{4,0},{6,2},{8,12},{10,14},{12,8},{14,10},{16,20},{18,... | collective-permute-start | bytes 2457608 | tf_op jit(solution)/shard_map/ppermute | solution.py:45
  90.2 0.0 collective-permute-done.8.refs_1_
  90.2 1.3 %shard_map.74 = f32[200,8,128]{2,1,0:T(8,128)S(1)} custom-call(f32[4,8,128]{2,1,0:T(8,128)S(1)} %shard_map.67.refs_0_, f32[201,8,128]{2,1,0:T(8,128)S(1)} %collective-permute-done.8.refs_1_, f32[200,8,128]{2,1,0:T(8,128)S(1)} %get-tuple-element.20.refs_2_), custom_call_target="tpu_custom_call" | custom-call | flops 1638400 | bytes 2457600 | tf_op jit(solution)/shard_map/pallas_call | solution.py:266
  91.5 2.6 %collective-permute-start.11 = (f32[200,8,128]{2,1,0:T(8,128)S(1)}, f32[200,8,128]{2,1,0:T(8,128)S(1)}, u32[]{:S(2)}, u32[]{:S(2)}) collective-permute-start(f32[200,8,128]{2,1,0:T(8,128)S(1)} %shard_map.74), channel_id=1, source_target_pairs={{0,8},{2,10},{8,16},{10,18},{12,4},{14,6},{16,24},{18,26},{20,12},... | collective-permute-start | bytes 2457608 | tf_op jit(solution)/shard_map/ppermute | solution.py:45
  94.1 0.0 collective-permute-done.1.refs_1_
  94.1 1.4 %shard_map.70 = f32[200,8,128]{2,1,0:T(8,128)S(1)} custom-call(f32[4,8,128]{2,1,0:T(8,128)S(1)} %shard_map.67.refs_0_, f32[201,8,128]{2,1,0:T(8,128)} %collective-permute-done.1.refs_1_, f32[200,8,128]{2,1,0:T(8,128)S(1)} %get-tuple-element.18.refs_2_), custom_call_target="tpu_custom_call" | custom-call | flops 1638400 | bytes 2457600 | tf_op jit(solution)/shard_map/pallas_call | solution.py:266
  95.5 0.2 collective-permute-start.7
  95.8 0.3 add_reduce_fusion
  96.1 0.1 multiply_reduce_fusion
  96.2 2.0 %collective-permute-done.12.refs_4_ = f32[200,8,128]{2,1,0:T(8,128)S(1)} collective-permute-done((f32[200,8,128]{2,1,0:T(8,128)S(1)}, f32[200,8,128]{2,1,0:T(8,128)S(1)}, u32[]{:S(2)}, u32[]{:S(2)}) %collective-permute-start.12) | collective-permute-done | bytes 819232 | tf_op jit(solution)/shard_map/ppermute | solution.py:45
  98.2 1.6 %shard_map.76.refs_0_ = f32[200,8,128]{2,1,0:T(8,128)S(1)} custom-call(f32[1,8,128]{2,1,0:T(8,128)S(1)} %copy-done.2, f32[201,8,128]{2,1,0:T(8,128)} %get-tuple-element.14.refs_0_.refs_1_, f32[201,8,128]{2,1,0:T(8,128)S(1)} %collective-permute-done.3.refs_2_, f32[201,8,128]{2,1,0:T(8,128)S(1)} %collective-permute-done.4.refs_3_, ...), custom_call_target="tpu_custom_call" | custom-call | flops 1638400 | bytes 4096000 | tf_op jit(solution)/shard_map/pallas_call | solution.py:266
  99.9 0.0 copy-start.3
  99.9 1.4 %shard_map.69.refs_0_ = f32[200,8,128]{2,1,0:T(8,128)S(1)} custom-call(f32[1,8,128]{2,1,0:T(8,128)S(1)} %copy-done.2, f32[201,8,128]{2,1,0:T(8,128)} %collective-permute-done.1.refs_1_, f32[200,8,128]{2,1,0:T(8,128)S(1)} %get-tuple-element.17.refs_2_), custom_call_target="tpu_custom_call" | custom-call | flops 1638400 | bytes 2457600 | tf_op jit(solution)/shard_map/pallas_call | solution.py:266
  101.3 0.8 collective-permute-done.10.refs_3_
  102.1 0.9 shard_map.73.refs_0_
  103.0 4.8 %collective-permute-done.15.refs_1_ = f32[200,8,128]{2,1,0:T(8,128)S(1)} collective-permute-done((f32[200,8,128]{2,1,0:T(8,128)S(1)}, f32[200,8,128]{2,1,0:T(8,128)S(1)}, u32[]{:S(2)}, u32[]{:S(2)}) %collective-permute-start.15) | collective-permute-done | bytes 819232 | tf_op jit(solution)/shard_map/ppermute | solution.py:45
  107.9 2.7 %shard_map.79.refs_2_ = f32[10,3,8,2560]{3,2,1,0:T(8,128)} custom-call(f32[1,8,128]{2,1,0:T(8,128)S(1)} %copy-done.2, s32[10]{0:T(128)S(1)} %copy-done.3, f32[3]{0:T(128)S(1)} %div.13.ratio, f32[200,8,128]{2,1,0:T(8,128)S(1)} %shard_map.76.refs_0_, f32[200,8,128]{2,1,0:T(8,128)S(1)} %collective-permute-done.15.refs_1_), custom_call_target="tpu_custom_call" | custom-call | flops 12288000 | bytes 2457600 | tf_op jit(solution)/shard_map/pallas_call | solution.py:359
  110.6 0.1 collective-permute-done.11.refs_1_
  110.7 2.7 %shard_map.80.refs_2_ = f32[10,3,8,2560]{3,2,1,0:T(8,128)} custom-call(f32[1,8,128]{2,1,0:T(8,128)S(1)} %copy-done.2, s32[10]{0:T(128)S(1)} %copy-done.3, f32[3]{0:T(128)S(1)} %div.13.ratio, f32[200,8,128]{2,1,0:T(8,128)S(1)} %shard_map.73.refs_0_, f32[200,8,128]{2,1,0:T(8,128)S(1)} %collective-permute-done.11.refs_1_, ...), custom_call_target="tpu_custom_call", output_to_operand_aliasing={{}: (5, {})} | custom-call | flops 12288000 | bytes 2457600 | tf_op jit(solution)/shard_map/pallas_call | solution.py:359
  113.4 1.7 %collective-permute-done.7.refs_1_ = f32[200,8,128]{2,1,0:T(8,128)S(1)} collective-permute-done((f32[200,8,128]{2,1,0:T(8,128)S(1)}, f32[200,8,128]{2,1,0:T(8,128)S(1)}, u32[]{:S(2)}, u32[]{:S(2)}) %collective-permute-start.7) | collective-permute-done | bytes 819232 | tf_op jit(solution)/shard_map/ppermute | solution.py:45
  115.1 2.7 %shard_map.81 = f32[10,3,8,2560]{3,2,1,0:T(8,128)} custom-call(f32[1,8,128]{2,1,0:T(8,128)S(1)} %copy-done.2, s32[10]{0:T(128)S(1)} %copy-done.3, f32[3]{0:T(128)S(1)} %div.13.ratio, f32[200,8,128]{2,1,0:T(8,128)S(1)} %shard_map.69.refs_0_, f32[200,8,128]{2,1,0:T(8,128)S(1)} %collective-permute-done.7.refs_1_, ...), custom_call_target="tpu_custom_call", output_to_operand_aliasing={{}: (5, {})} | custom-call | flops 12288000 | bytes 2457600 | tf_op jit(solution)/shard_map/pallas_call | solution.py:359
  (10 shorter events, 0.1 us)
Async XLA Ops:
  3.2 21.7 %collective-permute-start.3 = (f32[201,8,128]{2,1,0:T(8,128)}, f32[201,8,128]{2,1,0:T(8,128)S(1)}, u32[]{:S(2)}, u32[]{:S(2)}) collective-permute-start(f32[201,8,128]{2,1,0:T(8,128)} %get-tuple-element.14.refs_0_.refs_1_), channel_id=1, source_target_pairs={{0,8},{2,10},{4,12},{6,14},{8,0},{10,2},{12,4},{14,6},{16,24},{18,... | collective-permute-start | bytes 2469896 | tf_op jit(solution)/shard_map/ppermute | solution.py:45
  6.3 20.3 %collective-permute-start.4 = (f32[201,8,128]{2,1,0:T(8,128)}, f32[201,8,128]{2,1,0:T(8,128)S(1)}, u32[]{:S(2)}, u32[]{:S(2)}) collective-permute-start(f32[201,8,128]{2,1,0:T(8,128)} %get-tuple-element.14.refs_0_.refs_1_), channel_id=1, source_target_pairs={{8,16},{10,18},{12,20},{14,22},{16,8},{18,10},{20,12},{22,14},{9,1... | collective-permute-start | bytes 2469896 | tf_op jit(solution)/shard_map/ppermute | solution.py:45
  7.0 6.3 %collective-permute-start.13 = (f32[1,8,128]{2,1,0:T(8,128)}, f32[1,8,128]{2,1,0:T(8,128)S(1)}, u32[]{:S(2)}, u32[]{:S(2)}) collective-permute-start(f32[1,8,128]{2,1,0:T(8,128)} %get-tuple-element.13.refs_1_.refs_0_.plan), channel_id=1, source_target_pairs={{0,6},{2,4},{4,2},{6,0},{8,14},{10,12},{12,10},{14,8},{16,22},{18,... | collective-permute-start | bytes 12296 | tf_op jit(solution)/shard_map/ppermute | solution.py:45
  12.2 19.8 %collective-permute-start.2 = (f32[201,8,128]{2,1,0:T(8,128)}, f32[201,8,128]{2,1,0:T(8,128)S(1)}, u32[]{:S(2)}, u32[]{:S(2)}) collective-permute-start(f32[201,8,128]{2,1,0:T(8,128)} %get-tuple-element.15.refs_1_.refs_2_), channel_id=1, source_target_pairs={{0,2},{2,0},{4,6},{6,4},{8,10},{10,8},{12,14},{14,12},{16,18},{18,... | collective-permute-start | bytes 2469896 | tf_op jit(solution)/shard_map/ppermute | solution.py:45
  12.8 21.5 %collective-permute-start = (f32[201,8,128]{2,1,0:T(8,128)}, f32[201,8,128]{2,1,0:T(8,128)}, u32[]{:S(2)}, u32[]{:S(2)}) collective-permute-start(f32[201,8,128]{2,1,0:T(8,128)} %get-tuple-element.16.refs_2_), channel_id=1, source_target_pairs={{0,4},{2,6},{4,0},{6,2},{8,12},{10,14},{12,8},{14,10},{16,20},{18,... | collective-permute-start | bytes 2469896 | tf_op jit(solution)/shard_map/ppermute | solution.py:45
  13.4 38.5 %collective-permute-start.9 = (f32[201,8,128]{2,1,0:T(8,128)}, f32[201,8,128]{2,1,0:T(8,128)S(1)}, u32[]{:S(2)}, u32[]{:S(2)}) collective-permute-start(f32[201,8,128]{2,1,0:T(8,128)} %get-tuple-element.15.refs_1_.refs_2_), channel_id=1, source_target_pairs={{0,4},{2,6},{4,0},{6,2},{8,12},{10,14},{12,8},{14,10},{16,20},{18,... | collective-permute-start | bytes 2469896 | tf_op jit(solution)/shard_map/ppermute | solution.py:45
  24.9 52.7 %collective-permute-start.5 = (f32[201,8,128]{2,1,0:T(8,128)}, f32[201,8,128]{2,1,0:T(8,128)}, u32[]{:S(2)}, u32[]{:S(2)}) collective-permute-start(f32[201,8,128]{2,1,0:T(8,128)} %get-tuple-element.16.refs_2_), channel_id=1, source_target_pairs={{0,8},{2,10},{4,12},{6,14},{8,0},{10,2},{12,4},{14,6},{16,24},{18,... | collective-permute-start | bytes 2469896 | tf_op jit(solution)/shard_map/ppermute | solution.py:45
  26.6 51.6 %collective-permute-start.6 = (f32[201,8,128]{2,1,0:T(8,128)}, f32[201,8,128]{2,1,0:T(8,128)}, u32[]{:S(2)}, u32[]{:S(2)}) collective-permute-start(f32[201,8,128]{2,1,0:T(8,128)} %get-tuple-element.16.refs_2_), channel_id=1, source_target_pairs={{8,16},{10,18},{12,20},{14,22},{16,8},{18,10},{20,12},{22,14},{9,1... | collective-permute-start | bytes 2469896 | tf_op jit(solution)/shard_map/ppermute | solution.py:45
  32.0 58.1 %collective-permute-start.8 = (f32[201,8,128]{2,1,0:T(8,128)S(1)}, f32[201,8,128]{2,1,0:T(8,128)S(1)}, u32[]{:S(2)}, u32[]{:S(2)}) collective-permute-start(f32[201,8,128]{2,1,0:T(8,128)S(1)} %collective-permute-done.2.refs_0_.refs_3_.refs_2_), channel_id=1, source_target_pairs={{0,4},{2,6},{4,0},{6,2},{8,12},{10,14},{12,8},{14,10},{16,20},{18,... | collective-permute-start | bytes 2469896 | tf_op jit(solution)/shard_map/ppermute | solution.py:45
  34.4 59.8 %collective-permute-start.1 = (f32[201,8,128]{2,1,0:T(8,128)}, f32[201,8,128]{2,1,0:T(8,128)}, u32[]{:S(2)}, u32[]{:S(2)}) collective-permute-start(f32[201,8,128]{2,1,0:T(8,128)} %collective-permute-done.refs_1_.refs_3_), channel_id=1, source_target_pairs={{0,8},{2,10},{8,16},{10,18},{12,4},{14,6},{16,24},{18,26},{20,12},... | collective-permute-start | bytes 2469896 | tf_op jit(solution)/shard_map/ppermute | solution.py:45
  51.9 0.9 copy-start
  52.8 29.9 %collective-permute-start.14 = (f32[200,8,128]{2,1,0:T(8,128)}, f32[200,8,128]{2,1,0:T(8,128)}, u32[]{:S(2)}, u32[]{:S(2)}) collective-permute-start(f32[200,8,128]{2,1,0:T(8,128)} %shard_map.77), channel_id=1, source_target_pairs={{0,2},{2,0},{4,6},{6,4},{8,10},{10,8},{12,14},{14,12},{16,18},{18,... | collective-permute-start | bytes 2457608 | tf_op jit(solution)/shard_map/ppermute | solution.py:45
  56.8 13.5 %all-to-all-start = ((f32[32,1,128]{2,1,0:T(1,128)}), f32[32,1,128]{2,1,0:T(1,128)S(1)}, u32[]{:S(2)}, u32[]{:S(2)}) async-start(f32[32,1,128]{2,1,0:T(1,128)} %shard_map.66), calls=%async_computation | async-start | bytes 32768 | tf_op jit(solution)/shard_map/all_to_all | solution.py:183
  71.6 3.6 %copy-start.1 = (f32[201,8,128]{2,1,0:T(8,128)S(1)}, f32[201,8,128]{2,1,0:T(8,128)}, u32[]{:S(2)}) copy-start(f32[201,8,128]{2,1,0:T(8,128)} %copy-done) | copy-start | bytes 2469892
  71.6 3.6 %copy-start.2 = (f32[1,8,128]{2,1,0:T(8,128)S(1)}, f32[1,8,128]{2,1,0:T(8,128)}, u32[]{:S(2)}) copy-start(f32[1,8,128]{2,1,0:T(8,128)} %get-tuple-element.13.refs_1_.refs_0_.plan) | copy-start | bytes 12292
  77.6 20.6 %collective-permute-start.12 = (f32[200,8,128]{2,1,0:T(8,128)S(1)}, f32[200,8,128]{2,1,0:T(8,128)S(1)}, u32[]{:S(2)}, u32[]{:S(2)}) collective-permute-start(f32[200,8,128]{2,1,0:T(8,128)S(1)} %shard_map.75), channel_id=1, source_target_pairs={{0,2},{2,0},{4,6},{6,4},{8,10},{10,8},{12,14},{14,12},{16,18},{18,... | collective-permute-start | bytes 2457608 | tf_op jit(solution)/shard_map/ppermute | solution.py:45
  78.2 23.9 %collective-permute-start.10 = (f32[200,8,128]{2,1,0:T(8,128)S(1)}, f32[200,8,128]{2,1,0:T(8,128)S(1)}, u32[]{:S(2)}, u32[]{:S(2)}) collective-permute-start(f32[200,8,128]{2,1,0:T(8,128)S(1)} %shard_map.72), channel_id=1, source_target_pairs={{4,12},{6,14},{8,0},{10,2},{12,20},{14,22},{16,8},{18,10},{20,28},... | collective-permute-start | bytes 2457608 | tf_op jit(solution)/shard_map/ppermute | solution.py:45
  84.7 23.2 %collective-permute-start.15 = (f32[200,8,128]{2,1,0:T(8,128)S(1)}, f32[200,8,128]{2,1,0:T(8,128)S(1)}, u32[]{:S(2)}, u32[]{:S(2)}) collective-permute-start(f32[200,8,128]{2,1,0:T(8,128)S(1)} %shard_map.78), channel_id=1, source_target_pairs={{0,4},{2,6},{4,0},{6,2},{8,12},{10,14},{12,8},{14,10},{16,20},{18,... | collective-permute-start | bytes 2457608 | tf_op jit(solution)/shard_map/ppermute | solution.py:45
  91.5 19.2 %collective-permute-start.11 = (f32[200,8,128]{2,1,0:T(8,128)S(1)}, f32[200,8,128]{2,1,0:T(8,128)S(1)}, u32[]{:S(2)}, u32[]{:S(2)}) collective-permute-start(f32[200,8,128]{2,1,0:T(8,128)S(1)} %shard_map.74), channel_id=1, source_target_pairs={{0,8},{2,10},{8,16},{10,18},{12,4},{14,6},{16,24},{18,26},{20,12},... | collective-permute-start | bytes 2457608 | tf_op jit(solution)/shard_map/ppermute | solution.py:45
  95.5 19.6 %collective-permute-start.7 = (f32[200,8,128]{2,1,0:T(8,128)S(1)}, f32[200,8,128]{2,1,0:T(8,128)S(1)}, u32[]{:S(2)}, u32[]{:S(2)}) collective-permute-start(f32[200,8,128]{2,1,0:T(8,128)S(1)} %shard_map.70), channel_id=1, source_target_pairs={{0,2},{2,0},{4,6},{6,4},{8,10},{10,8},{12,14},{14,12},{16,18},{18,... | collective-permute-start | bytes 2457608 | tf_op jit(solution)/shard_map/ppermute | solution.py:45
  99.9 8.0 %copy-start.3 = (s32[10]{0:T(128)S(1)}, s32[10]{0:T(128)}, u32[]{:S(2)}) copy-start(s32[10]{0:T(128)} %shifts.5) | copy-start | bytes 124
